TPU v7x, 256 devices: a whole 4x4x8 slice. The times are simulated.
256 devices in a mesh: patch: 64 (over z, x, core), pair: 4 (over y).
Axes of the slice: x: 4, y: 4, z: 8, core: 2. Of those that a mesh axis runs over, the one named last changes fastest.
Arguments:
- node_latents: bfloat16 [65536, 1024], P('patch', 'pair'), may hold values from -12 to 12
- edge_latents: bfloat16 [131072, 1024], P('patch', 'pair'), may hold values from -12 to 12
- edge_sender: int32 [512, 256], P('patch'), may hold values from -1 to 2047, as said below
- edge_receiver: int32 [512, 256], P('patch'), may hold values from -1 to 31, as said below
- block_owner: int32 [512], P('patch'), may hold values from 0 to 63, as said below
- node_counts: int32 [64], P('patch'), may hold values from 512 to 1024, as said below
- halo_nodes: int32 [64, 64, 32], P('patch'), may hold values from 0 to 1023, as said below
- w_endpoints: bfloat16 [1024, 2, 1024], P(None, None, 'pair'), may hold values from -0.1875 to 0.1875
- w_edge_in: bfloat16 [1024, 1024], P(None, 'pair'), may hold values from -0.1875 to 0.1875
- edge_bias: float32 [1024], P('pair'), may hold values from -3 to 3
- w_edge_out: bfloat16 [1024, 1024], P('pair'), may hold values from -1 to 1
- edge_gain: float32 [1024], P('pair'), may hold values from 0.5 to 1.5
- edge_shift: float32 [1024], P('pair'), may hold values from -3 to 3
- w_node_in: bfloat16 [2, 1024, 1024], P(None, None, 'pair'), may hold values from -0.125 to 0.125
- node_bias: float32 [1024], P('pair'), may hold values from -3 to 3
- w_node_out: bfloat16 [1024, 1024], P('pair'), may hold values from -1 to 1
- node_gain: float32 [1024], P('pair'), may hold values from 0.5 to 1.5
- node_shift: float32 [1024], P('pair'), may hold values from -3 to 3
Outputs:
- updated_nodes: bfloat16 [65536, 1024], P('patch', 'pair')
- updated_edges: bfloat16 [131072, 1024], P('patch', 'pair')
Inputs may be any that keep to these rules, and one draw needn't show every extreme that they name: `edge_sender`: section q = slot // 32 of a patch's halo table holds, in order, the nodes halo_nodes[q, that patch]; -1 stands exactly where edge_receiver is -1. `edge_receiver`: -1 marks padding and stands only after the live edges of a block; within a block the live values never fall and take at most 16 distinct values; every patch has a block with 256 live edges and 16 distinct receivers. `block_owner`: no patch owns more than 1 of the blocks of one patch; every patch owns 1 of its own blocks, and some patch owns 1 block of every patch. `node_counts`: some patch has 1024 live nodes. halo_nodes[q, d] lists local live nodes of patch q (below node_counts[q]); entries may repeat.
All inputs are finite; a program needn't handle non-finite values.
Results may differ from a plain program's by a relative error of at most 0.008.
Values may be sent and summed in bfloat16 or wider, within the bound.
A program may use at most 128 MiB of HBM per device.

v0:
```python
import jax
import jax.numpy as jnp
from jax import lax
from jax.sharding import PartitionSpec as P

RT = 16


EPS = 1e-05


def in_order(tiles, dim):
    tiles = jnp.moveaxis(tiles, 0, dim)
    lengths = tiles.shape
    return tiles.reshape(*lengths[:dim], lengths[dim] * lengths[dim + 1], *lengths[dim + 2 :])


def copy_for_each(shard, axis):
    size = lax.axis_size(axis)
    return lax.all_to_all(
        jnp.broadcast_to(shard[None], (size, *shard.shape)), axis, 0, 0, tiled=True
    )


def collect(shard, axis, dim):
    return in_order(copy_for_each(shard, axis), dim)


def taken_together(shard, axis):
    everything = copy_for_each(shard, axis)
    return jnp.sum(everything, axis=0)


def packed_total(arrays, axis):
    flat, at, done = (jnp.concatenate([a.reshape(-1) for a in arrays]), 0, [])
    so_far = taken_together(flat, axis)
    for a in arrays:
        done.append(so_far[at : at + a.size].reshape(a.shape))
        at += a.size
    return tuple(done)


def in_blocks(shard, dim, size):
    before, after = (shard.shape[:dim], shard.shape[dim + 1 :])
    return jnp.moveaxis(shard.reshape(*before, size, -1, *after), dim, 0)


def sum_at_owner(shard, axis, dim):
    size = lax.axis_size(axis)
    tiles = lax.all_to_all(in_blocks(shard, dim, size), axis, 0, 0, tiled=True)
    return jnp.sum(tiles.astype(jnp.float32), axis=0)


def fold_product(weight, running, slab_rows):
    return running + jnp.dot(slab_rows, weight, preferred_element_type=jnp.float32)


def finish_norm(values, first_sum, second_sum, gain_row, shift_row, full_width):
    row_mean = first_sum[:, None] / full_width
    spread = second_sum[:, None] / full_width - row_mean * row_mean
    return (values - row_mean) * lax.rsqrt(spread + EPS) * gain_row[None, :] + shift_row[None, :]


def shards(
    node_latents,
    edge_latents,
    edge_sender,
    edge_receiver,
    block_owner,
    node_counts,
    halo_nodes,
    w_endpoints,
    w_edge_in,
    edge_bias,
    w_edge_out,
    edge_gain,
    edge_shift,
    w_node_in,
    node_bias,
    w_node_out,
    node_gain,
    node_shift,
):
    patches = lax.axis_size("patch")
    full_width = w_edge_in.shape[0]
    local_width = w_edge_in.shape[1]
    node_total = node_latents.shape[0]
    blocks = block_owner.shape[0]
    tile_size = edge_sender.shape[1]
    halo_size = halo_nodes.shape[2]
    capacity = max(1, blocks // patches)
    end_weight = w_endpoints.reshape(full_width, 2 * local_width)
    send_list = halo_nodes[0]
    full_nodes = collect(node_latents, "pair", 1)
    projected = jnp.dot(full_nodes, end_weight, preferred_element_type=jnp.float32).astype(
        jnp.bfloat16
    )
    picked = projected[send_list.reshape(-1)].reshape(patches, halo_size, 2 * local_width)
    halo_table = lax.all_to_all(picked, "patch", split_axis=0, concat_axis=0, tiled=True).reshape(
        patches * halo_size, 2 * local_width
    )
    halo_pairs = halo_table.reshape(patches * halo_size, 2, local_width)
    senders = edge_sender.reshape(-1)
    receivers = edge_receiver.reshape(-1)
    is_live = receivers >= 0
    edge_owner = jnp.repeat(block_owner, tile_size)
    sender_rows = halo_pairs[jnp.maximum(senders, 0), 0]
    receiver_rows = halo_pairs[edge_owner * halo_size + jnp.maximum(receivers, 0), 1]
    start_value = (
        sender_rows.astype(jnp.float32) + receiver_rows.astype(jnp.float32) + edge_bias[None, :]
    )
    edge_pre = fold_product(
        w_edge_in, start_value, lax.all_gather(edge_latents, "pair", axis=1, tiled=True)
    )
    edge_hidden = jax.nn.silu(edge_pre).astype(jnp.bfloat16)
    edge_terms = jnp.dot(edge_hidden, w_edge_out, preferred_element_type=jnp.float32)
    edge_mixed = lax.psum_scatter(
        edge_terms.astype(jnp.bfloat16), "pair", scatter_dimension=1, tiled=True
    ).astype(jnp.float32)
    edge_first, edge_second = packed_total(
        (jnp.sum(edge_mixed, axis=1), jnp.sum(edge_mixed * edge_mixed, axis=1)), "pair"
    )
    edge_norm = finish_norm(edge_mixed, edge_first, edge_second, edge_gain, edge_shift, full_width)
    old_edges = edge_latents.astype(jnp.float32)
    new_edges = jnp.where(is_live[:, None], old_edges + edge_norm, old_edges).astype(jnp.bfloat16)
    same_owner = block_owner[:, None] == block_owner[None, :]
    earlier = jnp.arange(blocks)[None, :] < jnp.arange(blocks)[:, None]
    slot_rank = jnp.sum((same_owner & earlier).astype(jnp.int32), axis=1)
    target_slot = block_owner * capacity + slot_rank
    kept_rows = jnp.where(is_live[:, None], new_edges, jnp.zeros_like(new_edges)).reshape(
        blocks, tile_size, local_width
    )
    previous = jnp.concatenate(
        [jnp.full((blocks, 1), -2, jnp.int32), edge_receiver[:, :-1]], axis=1
    )
    segment = jnp.cumsum((edge_receiver != previous).astype(jnp.int32), axis=1) - 1
    segment = jnp.where(edge_receiver >= 0, segment, RT)
    member = segment[:, None, :] == jnp.arange(RT, dtype=jnp.int32)[None, :, None]
    tile_sums = jnp.einsum(
        "brt,btd->brd", member.astype(jnp.bfloat16), kept_rows, preferred_element_type=jnp.float32
    )
    tile_ids = jnp.max(jnp.where(member, edge_receiver[:, None, :], -1), axis=2)
    send_values = (
        jnp.zeros((patches * capacity, RT, local_width), jnp.float32).at[target_slot].set(tile_sums)
    )
    send_ids = jnp.full((patches * capacity, RT), -1, jnp.int32).at[target_slot].set(tile_ids)
    got_values, got_ids = (
        lax.all_to_all(
            send_values.astype(jnp.bfloat16), "patch", split_axis=0, concat_axis=0, tiled=True
        ).astype(send_values.dtype),
        lax.all_to_all(send_ids, "patch", split_axis=0, concat_axis=0, tiled=True),
    )
    source = (jnp.arange(patches * capacity, dtype=jnp.int32) // capacity)[:, None]
    node_index = send_list[source, jnp.maximum(got_ids, 0)]
    node_index = jnp.where(got_ids >= 0, node_index, node_total)
    aggregate = jax.ops.segment_sum(
        got_values.reshape(-1, local_width), node_index.reshape(-1), num_segments=node_total + 1
    )
    aggregated = aggregate[:node_total].astype(jnp.bfloat16)
    node_start = (
        jnp.dot(full_nodes, w_node_in[0], preferred_element_type=jnp.float32) + node_bias[None, :]
    )
    node_pre = fold_product(w_node_in[1], node_start, collect(aggregated, "pair", 1))
    node_hidden = jax.nn.silu(node_pre).astype(jnp.bfloat16)
    node_terms = jnp.dot(node_hidden, w_node_out, preferred_element_type=jnp.float32)
    node_mixed = sum_at_owner(node_terms.astype(jnp.bfloat16), "pair", 1)
    node_first, node_second = packed_total(
        (jnp.sum(node_mixed, axis=1), jnp.sum(node_mixed * node_mixed, axis=1)), "pair"
    )
    node_norm = finish_norm(node_mixed, node_first, node_second, node_gain, node_shift, full_width)
    live_nodes = jnp.arange(node_total, dtype=jnp.int32) < node_counts[0]
    old_nodes = node_latents.astype(jnp.float32)
    updated_nodes = jnp.where(live_nodes[:, None], old_nodes + node_norm, old_nodes).astype(
        jnp.bfloat16
    )
    return (updated_nodes, new_edges)


def solution(mesh):
    return jax.shard_map(
        shards,
        mesh=mesh,
        in_specs=(
            P("patch", "pair"),
            P("patch", "pair"),
            P("patch", None),
            P("patch", None),
            P("patch"),
            P("patch"),
            P("patch", None, None),
            P(None, None, "pair"),
            P(None, "pair"),
            P("pair"),
            P("pair", None),
            P("pair"),
            P("pair"),
            P(None, None, "pair"),
            P("pair"),
            P("pair", None),
            P("pair"),
            P("pair"),
        ),
        out_specs=(P("patch", "pair"), P("patch", "pair")),
        check_vma=False,
    )
```

profile of v0, /device:TPU:1, one launch (start us, length us, event | category | flops | bytes accessed | tf_op | source)
XLA Modules:
  0.0 377.4 jit_solution(2874348802031950959)
XLA Ops:
  7.2 0.7 all-gather.2.cloned.1.call-update
  7.9 1.2 copy.35
  9.2 1.6 broadcast_in_dim.61
  10.8 5.0 %all-to-all-start = ((bf16[4,1024,256]{1,2,0:T(8,128)(2,1)}), bf16[4,1024,256]{1,2,0:T(8,128)(2,1)S(1)}, u32[]{:S(2)}, u32[]{:S(2)}) async-start(bf16[4,1024,256]{1,2,0:T(8,128)(2,1)} %broadcast_in_dim.61), calls=%async_computation | async-start | bytes 4194304 | tf_op jit(solution)/shard_map/all_to_all | solution.py:20
  15.8 2.4 copy.48
  18.4 31.5 %all-to-all-done = bf16[4,1024,256]{1,2,0:T(8,128)(2,1)S(1)} async-done(((bf16[4,1024,256]{1,2,0:T(8,128)(2,1)}), bf16[4,1024,256]{1,2,0:T(8,128)(2,1)S(1)}, u32[]{:S(2)}, u32[]{:S(2)}) %all-to-all-start) | async-done | bytes 2097184 | tf_op jit(solution)/shard_map/all_to_all | solution.py:20
  49.9 1.4 copy-done.4
  51.3 3.1 convolution_convert_fusion.2
  54.4 9.2 %gather_fusion.1 = bf16[2048,512]{1,0:T(8,128)(2,1)} fusion(bf16[1024,512]{1,0:T(8,128)(2,1)S(1)} %convolution_convert_fusion.2, s32[2048]{0:T(1024)S(1)} %broadcast_clamp_fusion), kind=kCustom, calls=%fused_computation.1 | custom fusion | bytes 4202496 | tf_op jit(solution)/shard_map/gather | solution.py:98
  63.6 16.2 %all-to-all-start.2 = ((bf16[64,32,512]{2,1,0:T(8,128)(2,1)}), bf16[64,32,512]{2,1,0:T(8,128)(2,1)}, u32[]{:S(2)}, u32[]{:S(2)}) async-start(bf16[64,32,512]{2,1,0:T(8,128)(2,1)} %bitcast.58), calls=%async_computation.2 | async-start | bytes 4194304 | tf_op jit(solution)/shard_map/all_to_all | solution.py:99
  80.0 0.6 reduce-window.6
  80.6 0.2 slice_reduce_fusion
  81.2 48.3 %all-to-all-done.2 = bf16[64,32,512]{2,1,0:T(8,128)(2,1)} async-done(((bf16[64,32,512]{2,1,0:T(8,128)(2,1)}), bf16[64,32,512]{2,1,0:T(8,128)(2,1)}, u32[]{:S(2)}, u32[]{:S(2)}) %all-to-all-start.2) | async-done | bytes 2097184 | tf_op jit(solution)/shard_map/all_to_all | solution.py:99
  129.5 2.5 reshape_reshape.3
  132.0 20.5 %gather_fusion.3 = bf16[2048,256]{1,0:T(8,128)(2,1)} fusion(bf16[2048,2,256]{2,1,0:T(2,128)(2,1)S(1)} %reshape_reshape.3, s32[2048]{0:T(1024)S(1)} %bitcast.57), kind=kCustom, calls=%fused_computation.3 | custom fusion | bytes 2113536 | tf_op jit(solution)/shard_map/gather | solution.py:108
  152.5 20.3 %gather_fusion.2 = bf16[2048,256]{1,0:T(8,128)(2,1)} fusion(bf16[2048,2,256]{2,1,0:T(2,128)(2,1)S(1)} %reshape_reshape.3, s32[2048]{0:T(1024)S(1)} %bitcast.56), kind=kCustom, calls=%fused_computation.2 | custom fusion | bytes 2113536 | tf_op jit(solution)/shard_map/gather | solution.py:107
  172.8 9.3 %convolution_convert_fusion = bf16[2048,1024]{1,0:T(8,128)(2,1)} fusion(bf16[256,1024]{1,0:T(8,128)(2,1)S(1)} %copy-done, bf16[2048,1024]{1,0:T(8,128)(2,1)} %all-gather.2.cloned.1.call-done, bf16[1024,256]{1,0:T(8,128)(2,1)} %param.26, bf16[2048,256]{1,0:T(8,128)(2,1)} %gather_fusion.3, bf16[2048,256]{1,0:T(8,128)(2,1)} %gather_fusion.2, f32[256]{0:T(256)S(1)} %copy-done.13), kind=kOutput, calls=%fused_computation.9 | convolution fusion | flops 2154823680 | bytes 11535360 | tf_op jit(solution)/shard_map/dot_general | solution.py:116
  182.2 45.3 %reduce-scatter.2.cloned.1.call-done = bf16[2048,256]{1,0:T(8,128)(2,1)} async-done(((bf16[2048,1024]{1,0:T(8,128)(2,1)}), bf16[2048,256]{1,0:T(8,128)(2,1)}) %reduce-scatter.2.cloned.1.call-update) | async-done | bytes 1048592 | tf_op jit(solution)/shard_map/reduce_scatter | solution.py:117
  227.4 1.9 convert_reduce_fusion.2
  229.4 0.7 broadcast_in_dim.74
  230.0 3.3 all-to-all-start.3
  233.3 0.2 select_reduce_fusion
  233.6 1.2 scatter_custom_fusion
  234.7 3.0 all-to-all-done.3
  237.8 11.9 %all-to-all-start.1 = ((s32[64,1,16]{2,1,0:T(1,128)}), s32[64,1,16]{2,1,0:T(1,128)S(1)}, u32[]{:S(2)}, u32[]{:S(2)}) async-start(s32[64,1,16]{2,1,0:T(1,128)} %bitcast.6), calls=%async_computation.1 | async-start | bytes 65536 | tf_op jit(solution)/shard_map/all_to_all | solution.py:151
  249.8 2.6 broadcast_select_fusion
  252.4 0.2 fusion.18
  252.8 0.7 scatter_fusion
  253.5 0.9 convert_element_type.59
  254.4 4.7 %all-to-all-done.1 = s32[64,1,16]{2,1,0:T(1,128)S(1)} async-done(((s32[64,1,16]{2,1,0:T(1,128)}), s32[64,1,16]{2,1,0:T(1,128)S(1)}, u32[]{:S(2)}, u32[]{:S(2)}) %all-to-all-start.1) | async-done | bytes 4128 | tf_op jit(solution)/shard_map/all_to_all | solution.py:151
  259.1 5.6 %all-to-all-start.4 = ((bf16[64,16,256]{2,1,0:T(8,128)(2,1)}), bf16[64,16,256]{2,1,0:T(8,128)(2,1)S(1)}, u32[]{:S(2)}, u32[]{:S(2)}) async-start(bf16[64,16,256]{2,1,0:T(8,128)(2,1)} %convert_element_type.59), calls=%async_computation.5 | async-start | bytes 1048576 | tf_op jit(solution)/shard_map/all_to_all | solution.py:148
  265.0 7.3 %gather_fusion = s32[1024]{0:T(1024)S(1)} fusion(s32[64,32]{0,1:T(8,128)S(1)} %bitcast.55, s32[1024]{0:T(1024)S(1)} %reshape.228), kind=kCustom, calls=%fused_computation | custom fusion | bytes 16384 | tf_op jit(solution)/shard_map/gather | solution.py:154
  272.4 10.0 %all-to-all-done.4 = bf16[64,16,256]{2,1,0:T(8,128)(2,1)S(1)} async-done(((bf16[64,16,256]{2,1,0:T(8,128)(2,1)}), bf16[64,16,256]{2,1,0:T(8,128)(2,1)S(1)}, u32[]{:S(2)}, u32[]{:S(2)}) %all-to-all-start.4) | async-done | bytes 524320 | tf_op jit(solution)/shard_map/all_to_all | solution.py:148
  282.4 7.8 %scatter_custom_fusion.2 = f32[1025,256]{1,0:T(8,128)S(1)} fusion(s32[1024]{0:T(1024)S(1)} %bitcast.70, bf16[1024,256]{1,0:T(8,128)(2,1)S(1)} %bitcast.62, f32[]{:T(128)} %constant.20.clone.1), kind=kCustom, calls=%fused_computation.28 | custom fusion | flops 524288 | bytes 1573892 | tf_op jit(solution)/shard_map/scatter-add | solution.py:156
  290.2 0.2 copy.39
  290.4 1.6 broadcast_in_dim.76
  292.0 4.6 %all-to-all-start.5 = ((bf16[4,1024,256]{1,2,0:T(8,128)(2,1)}), bf16[4,1024,256]{1,2,0:T(8,128)(2,1)}, u32[]{:S(2)}, u32[]{:S(2)}) async-start(bf16[4,1024,256]{1,2,0:T(8,128)(2,1)} %broadcast_in_dim.76), calls=%async_computation.6 | async-start | bytes 4194304 | tf_op jit(solution)/shard_map/all_to_all | solution.py:20
  296.6 2.8 convolution_add_fusion.2
  299.4 23.4 %all-to-all-done.5 = bf16[4,1024,256]{1,2,0:T(8,128)(2,1)} async-done(((bf16[4,1024,256]{1,2,0:T(8,128)(2,1)}), bf16[4,1024,256]{1,2,0:T(8,128)(2,1)}, u32[]{:S(2)}, u32[]{:S(2)}) %all-to-all-start.5) | async-done | bytes 2097184 | tf_op jit(solution)/shard_map/all_to_all | solution.py:20
  322.8 5.7 %convolution_convert_fusion.1 = bf16[1024,1024]{0,1:T(8,128)(2,1)} fusion(bf16[256,1024]{1,0:T(8,128)(2,1)} %param.33, f32[1024,256]{1,0:T(8,128)} %convolution_add_fusion.2, bf16[1024,1024]{0,1:T(8,128)(2,1)} %bitcast.18, bf16[2,1024,256]{2,1,0:T(8,128)(2,1)} %param.31), kind=kOutput, calls=%fused_computation.21 | convolution fusion | flops 1076363264 | bytes 6291456 | tf_op jit(solution)/shard_map/dot_general | solution.py:165
  328.5 4.4 %all-to-all-start.6 = ((bf16[4,1024,256]{1,2,0:T(8,128)(2,1)}), bf16[4,1024,256]{1,2,0:T(8,128)(2,1)}, u32[]{:S(2)}, u32[]{:S(2)}) async-start(bf16[4,1024,256]{1,2,0:T(8,128)(2,1)} %bitcast.21), calls=%async_computation.7 | async-start | bytes 4194304 | tf_op jit(solution)/shard_map/all_to_all | solution.py:50
  333.6 24.7 %all-to-all-done.6 = bf16[4,1024,256]{1,2,0:T(8,128)(2,1)} async-done(((bf16[4,1024,256]{1,2,0:T(8,128)(2,1)}), bf16[4,1024,256]{1,2,0:T(8,128)(2,1)}, u32[]{:S(2)}, u32[]{:S(2)}) %all-to-all-start.6) | async-done | bytes 2097184 | tf_op jit(solution)/shard_map/all_to_all | solution.py:50
  358.2 2.7 convert_reduce_fusion
  361.0 0.6 broadcast_in_dim.77
  361.7 3.3 all-to-all-start.7
  364.9 4.3 %all-to-all-done.7 = f32[4,1,2048]{2,1,0:T(1,128)S(1)} async-done(((f32[4,1,2048]{2,1,0:T(1,128)}), f32[4,1,2048]{2,1,0:T(1,128)S(1)}, u32[]{:S(2)}, u32[]{:S(2)}) %all-to-all-start.7) | async-done | bytes 32800 | tf_op jit(solution)/shard_map/all_to_all | solution.py:20
  369.3 0.3 fusion.5
  369.6 1.0 copy.41
  (64 shorter events, 1.5 us)
Async XLA Ops:
  7.2 165.7 %copy-start = (bf16[256,1024]{1,0:T(8,128)(2,1)S(1)}, bf16[256,1024]{1,0:T(8,128)(2,1)}, u32[]{:S(2)}) copy-start(bf16[256,1024]{1,0:T(8,128)(2,1)} %param.28) | copy-start | bytes 1572868
  7.2 165.6 %all-gather.2.cloned.1.call-start = ((), (), s32[]{:S(2)}) async-start(), calls=%async_computation.9 | async-start | bytes 5242880 | tf_op jit(solution)/shard_map/all_gather | solution.py:113
  10.8 39.1 %all-to-all-start = ((bf16[4,1024,256]{1,2,0:T(8,128)(2,1)}), bf16[4,1024,256]{1,2,0:T(8,128)(2,1)S(1)}, u32[]{:S(2)}, u32[]{:S(2)}) async-start(bf16[4,1024,256]{1,2,0:T(8,128)(2,1)} %broadcast_in_dim.61), calls=%async_computation | async-start | bytes 4194304 | tf_op jit(solution)/shard_map/all_to_all | solution.py:20
  15.8 2.4 copy-start.1
  49.9 1.4 copy-start.4
  63.6 16.3 %copy-start.6 = (s32[8,256]{1,0:T(8,128)S(1)}, s32[8,256]{1,0:T(8,128)}, u32[]{:S(2)}) copy-start(s32[8,256]{1,0:T(8,128)} %param.21) | copy-start | bytes 24580
  63.6 17.2 %copy-start.12 = (s32[8]{0:T(128)S(1)}, s32[8]{0:T(128)}, u32[]{:S(2)}) copy-start(s32[8]{0:T(128)} %param.22) | copy-start | bytes 100
  63.6 17.5 %copy-start.7 = (s32[8,256]{1,0:T(8,128)S(1)}, s32[8,256]{1,0:T(8,128)}, u32[]{:S(2)}) copy-start(s32[8,256]{1,0:T(8,128)} %param.20) | copy-start | bytes 24580
  63.6 65.9 %all-to-all-start.2 = ((bf16[64,32,512]{2,1,0:T(8,128)(2,1)}), bf16[64,32,512]{2,1,0:T(8,128)(2,1)}, u32[]{:S(2)}, u32[]{:S(2)}) async-start(bf16[64,32,512]{2,1,0:T(8,128)(2,1)} %bitcast.58), calls=%async_computation.2 | async-start | bytes 4194304 | tf_op jit(solution)/shard_map/all_to_all | solution.py:99
  79.9 147.6 %reduce-scatter.2.cloned.1.call-start = ((), (), s32[]{:S(2)}) async-start(), calls=%async_computation.10 | async-start | bytes 5242880 | tf_op jit(solution)/shard_map/reduce_scatter | solution.py:117
  152.5 20.3 %copy-start.13 = (f32[256]{0:T(256)S(1)}, f32[256]{0:T(256)}, u32[]{:S(2)}) copy-start(f32[256]{0:T(256)} %param.27) | copy-start | bytes 3076
  182.1 67.6 %copy-start.2 = (bf16[2048,256]{1,0:T(8,128)(2,1)S(1)}, bf16[2048,256]{1,0:T(8,128)(2,1)}, u32[]{:S(2)}) copy-start(bf16[2048,256]{1,0:T(8,128)(2,1)} %param.19) | copy-start | bytes 3145732
  182.1 67.6 %copy-start.8 = (f32[256]{0:T(256)S(1)}, f32[256]{0:T(256)}, u32[]{:S(2)}) copy-start(f32[256]{0:T(256)} %param.30) | copy-start | bytes 3076
  182.1 67.6 %copy-start.9 = (f32[256]{0:T(256)S(1)}, f32[256]{0:T(256)}, u32[]{:S(2)}) copy-start(f32[256]{0:T(256)} %param.29) | copy-start | bytes 3076
  227.4 22.4 %copy-start.3 = (bf16[2048,256]{1,0:T(8,128)(2,1)S(1)}, bf16[2048,256]{1,0:T(8,128)(2,1)}, u32[]{:S(2)}) copy-start(bf16[2048,256]{1,0:T(8,128)(2,1)} %reduce-scatter.2.cloned.1.call-done) | copy-start | bytes 3145732
  230.0 7.7 %all-to-all-start.3 = ((f32[4,1,4096]{2,1,0:T(1,128)}), f32[4,1,4096]{2,1,0:T(1,128)S(1)}, u32[]{:S(2)}, u32[]{:S(2)}) async-start(f32[4,1,4096]{2,1,0:T(1,128)} %broadcast_in_dim.74), calls=%async_computation.4 | async-start | bytes 131072 | tf_op jit(solution)/shard_map/all_to_all | solution.py:20
  237.8 21.3 %all-to-all-start.1 = ((s32[64,1,16]{2,1,0:T(1,128)}), s32[64,1,16]{2,1,0:T(1,128)S(1)}, u32[]{:S(2)}, u32[]{:S(2)}) async-start(s32[64,1,16]{2,1,0:T(1,128)} %bitcast.6), calls=%async_computation.1 | async-start | bytes 65536 | tf_op jit(solution)/shard_map/all_to_all | solution.py:151
  259.1 23.3 %all-to-all-start.4 = ((bf16[64,16,256]{2,1,0:T(8,128)(2,1)}), bf16[64,16,256]{2,1,0:T(8,128)(2,1)S(1)}, u32[]{:S(2)}, u32[]{:S(2)}) async-start(bf16[64,16,256]{2,1,0:T(8,128)(2,1)} %convert_element_type.59), calls=%async_computation.5 | async-start | bytes 1048576 | tf_op jit(solution)/shard_map/all_to_all | solution.py:148
  292.0 4.6 %copy-start.5 = (bf16[4,1024,256]{1,2,0:T(8,128)(2,1)S(1)}, bf16[4,1024,256]{1,2,0:T(8,128)(2,1)}, u32[]{:S(2)}) copy-start(bf16[4,1024,256]{1,2,0:T(8,128)(2,1)} %copy-done.4) | copy-start | bytes 6291460
  292.0 4.6 %copy-start.14 = (f32[256]{0:T(256)S(1)}, f32[256]{0:T(256)}, u32[]{:S(2)}) copy-start(f32[256]{0:T(256)} %param.32) | copy-start | bytes 3076
  292.0 30.8 %all-to-all-start.5 = ((bf16[4,1024,256]{1,2,0:T(8,128)(2,1)}), bf16[4,1024,256]{1,2,0:T(8,128)(2,1)}, u32[]{:S(2)}, u32[]{:S(2)}) async-start(bf16[4,1024,256]{1,2,0:T(8,128)(2,1)} %broadcast_in_dim.76), calls=%async_computation.6 | async-start | bytes 4194304 | tf_op jit(solution)/shard_map/all_to_all | solution.py:20
  328.5 29.8 %all-to-all-start.6 = ((bf16[4,1024,256]{1,2,0:T(8,128)(2,1)}), bf16[4,1024,256]{1,2,0:T(8,128)(2,1)}, u32[]{:S(2)}, u32[]{:S(2)}) async-start(bf16[4,1024,256]{1,2,0:T(8,128)(2,1)} %bitcast.21), calls=%async_computation.7 | async-start | bytes 4194304 | tf_op jit(solution)/shard_map/all_to_all | solution.py:50
  333.5 35.7 %copy-start.10 = (f32[256]{0:T(256)S(1)}, f32[256]{0:T(256)}, u32[]{:S(2)}) copy-start(f32[256]{0:T(256)} %param.35) | copy-start | bytes 3076
  333.6 35.7 %copy-start.11 = (f32[256]{0:T(256)S(1)}, f32[256]{0:T(256)}, u32[]{:S(2)}) copy-start(f32[256]{0:T(256)} %param.34) | copy-start | bytes 3076
  361.7 7.5 %all-to-all-start.7 = ((f32[4,1,2048]{2,1,0:T(1,128)}), f32[4,1,2048]{2,1,0:T(1,128)S(1)}, u32[]{:S(2)}, u32[]{:S(2)}) async-start(f32[4,1,2048]{2,1,0:T(1,128)} %broadcast_in_dim.77), calls=%async_computation.8 | async-start | bytes 65536 | tf_op jit(solution)/shard_map/all_to_all | solution.py:20
Sparse Core Ops, SparseCore 0:
  9.8 67.8 all-gather.1
  182.3 45.0 reduce-scatter.1
where the time goes:
time: 380 us; the launch traced here: 377 us
  waiting for transfers between devices  196 us (52%)
  local copies, waits for them, and re-layouts  73.2 us (19%)
  starting transfers between devices  54.4 us (14%)
  matrix products  21.2 us (6%)
  other arithmetic  17.8 us (5%)
  between operations  15.1 us (4%)
    all_to_all x4, waiting for transfers between devices, copy_for_each(): lax.all_to_all(jnp.broadcast_to(shard[None], (size, *shard.shape)), axis,...  62.2 us
    all_to_all x1, waiting for transfers between devices, shards(): lax.all_to_all(picked, 'patch', split_axis=0, concat_axis=0, tiled=True)  48.3 us
    reduce_scatter x1, waiting for transfers between devices, shards(): lax.psum_scatter(edge_terms.astype(jnp.bfloat16), 'pair', scatter_dimensi...  45.3 us
    all_to_all x1, waiting for transfers between devices, sum_at_owner(): tiles = lax.all_to_all(in_blocks(shard, dim, size), axis, 0, 0, tiled=True)  24.7 us
    gather x1, local copies, waits for them, and re-layouts, shards(): halo_pairs[edge_owner * halo_size + jnp.maximum(receivers, 0), 1]  20.5 us
    gather x1, local copies, waits for them, and re-layouts, shards(): sender_rows = halo_pairs[jnp.maximum(senders, 0), 0]  20.3 us
    all_to_all x1, starting transfers between devices, shards(): lax.all_to_all(picked, 'patch', split_axis=0, concat_axis=0, tiled=True)  16.2 us
    all_to_all x4, starting transfers between devices, copy_for_each(): lax.all_to_all(jnp.broadcast_to(shard[None], (size, *shard.shape)), axis,...  16.1 us
  transfers between devices with their start and end apart: 10, of which 9 were waited for; matrix products, arithmetic and copies ran while one was open for 21% of the time, Pallas kernels for 0%

commit v1 on v0

v1 whole, which is shorter than its diff:
```python
import jax
import jax.numpy as jnp
from jax import lax
from jax.experimental import pallas as pl
from jax.experimental.pallas import tpu as pltpu
from jax.sharding import PartitionSpec as P

EPS = 1e-05
MESH = pl.DeviceIdType.MESH
BF = jnp.bfloat16
F32 = jnp.float32
I32 = jnp.int32

NODE = 1024
EDGE = 2048
FEAT = 256
WIDE = 1024
PATCH = 64
HALO = 32
RT = 16
BLK = 8
TILE = 256
ROWS = 2 * TILE
SEL = ROWS + 2 * HALO
NROW = NODE // 4
ANY = pl.BlockSpec(memory_space=pl.ANY)
VM = pl.BlockSpec(memory_space=pltpu.VMEM)
SM = pl.BlockSpec(memory_space=pltpu.SMEM)


def iota(shape, dim):
    return lax.broadcasted_iota(I32, shape, dim)


def hot(mask):
    return jnp.where(mask, 1.0, 0.0).astype(BF)


def dot(a, b):
    return jnp.dot(a, b, preferred_element_type=F32)


def silu(v):
    return v / (1.0 + jnp.exp(-v))


def aligned(v, n):
    return pl.multiple_of(v, n)


def kernel(
    nl, el, snd, rcv, own, cnt, hal, wep, win, eb, wout, eg, es, wnin, nb, wnout, ng, ns,
    o_n, o_e,
    nl_v, pcol, picked, halo_r, idcol, rcol, idt, rank8, idr, vec, gacc, sbuf, xs,
    xe, xn, wa, wb, acc, hid, outb, tsb, tsr, sv, vv, amat, abuf, xa, acc2, outn,
    loc, hs, hr, ids_s, ids_r, es_, er_, xns, xnr, vs, vr,
    wys, wyr, wxs, wxr, wds, wdr, ss, sr, tss, tsrr, v2s, v2r, as_, ar_, oes, oer, ons, onr,
):
    me = lax.axis_index("patch")
    j = lax.axis_index("pair")
    z, x, c = me // 8, lax.rem(me // 2, 4), lax.rem(me, 2)

    def dz_of(m):
        odd = lax.rem(m, 2)
        return lax.rem(odd * ((m + 1) // 2) + (1 - odd) * (8 - m // 2), 8)

    def place(m, t):
        return lax.rem(x + t // 2, 4) * 2 + lax.rem(c + lax.rem(t, 2), 2)

    def dest(m, t):
        return lax.rem(z + dz_of(m), 8) * 8 + place(m, t)

    def rem(src, dst, s, r, dev):
        return pltpu.make_async_remote_copy(
            src_ref=src, dst_ref=dst, send_sem=s, recv_sem=r, device_id=dev, device_id_type=MESH
        )

    def pair_of(dy):
        return lax.rem(j + dy, 4)

    loads = []

    def load(src, dst):
        copy = pltpu.make_async_copy(src, dst, loc.at[len(loads)])
        copy.start()
        loads.append(copy)
        return copy

    ld_nl = load(nl, nl_v)
    ld_e = [load(win, wa.at[0, 0]), load(wep.at[0], wa.at[0, 1]), load(wep.at[1], wa.at[0, 2])]
    ld_e.append(load(wout, wb.at[0, 0]))
    my_cols = pl.ds(aligned(j * FEAT, FEAT), FEAT)
    my_edges = pl.ds(aligned(j * ROWS, ROWS), ROWS)
    my_nodes = pl.ds(aligned(j * NROW, NROW), NROW)
    ld_x = [load(el.at[my_edges], xe.at[:, my_cols]), load(nl.at[my_nodes], xn.at[:, my_cols])]
    ld_n = [load(wnin.at[0], wa.at[0, 3]), load(wnin.at[1], wa.at[0, 4]), load(wnout, wb.at[0, 1])]

    barrier = pltpu.get_barrier_semaphore()

    def greet(r, carry):
        pl.semaphore_signal(
            barrier, inc=1, device_id=(dest(r // 8, lax.rem(r, 8)), j), device_id_type=MESH
        )
        return carry

    lax.fori_loop(1, PATCH, greet, 0)
    for dy in (1, 2, 3):
        pl.semaphore_signal(barrier, inc=1, device_id=(me, pair_of(dy)), device_id_type=MESH)

    hal_t = jnp.concatenate([hal[0], jnp.zeros((PATCH, 128 - HALO), I32)], axis=1).T
    for d in range(PATCH):
        pcol[d * HALO : (d + 1) * HALO, :] = hal_t[0:HALO, d : d + 1]
    ld_nl.wait()

    def pick(m):
        base = aligned(lax.rem(z + dz_of(m), 8) * 256, 256)
        ones = hot(pcol[pl.ds(base, 256), :] == iota((256, NODE), 1))
        picked[pl.ds(aligned(m * 256, 256), 256), :] = dot(ones, nl_v[...]).astype(BF)

    def halo_copy(m, t):
        return rem(
            picked.at[pl.ds(aligned(m * 256 + place(m, t) * HALO, HALO), HALO)],
            halo_r.at[pl.ds(aligned((m * 8 + t) * HALO, HALO), HALO)],
            hs,
            hr.at[m // 2],
            (dest(m, t), j),
        )

    pick(0)
    pl.semaphore_wait(barrier, PATCH - 1 + 3)

    row_a = pl.ds(aligned((c * 4 + x) * 128, 128), 128)
    row_b = pl.ds(aligned((c * 4 + x) * 32, 32), 32)
    units = ((0, 3, 0), (3, 2, 1))

    def weights_y(k):
        first, count, b = units[k]
        copies = []
        for dy in (2, 1, 3):
            dev = (me, pair_of(dy))
            i = dy - 1
            copies.append(rem(
                wa.at[0, pl.ds(first, count), row_a], wa.at[4 - dy, pl.ds(first, count), row_a],
                wys.at[2 * k, i], wyr.at[2 * k, i], dev,
            ))
            copies.append(rem(
                wb.at[0, b, row_b], wb.at[4 - dy, b, row_b],
                wys.at[2 * k + 1, i], wyr.at[2 * k + 1, i], dev,
            ))
        return copies

    def weights_x(k):
        first, count, b = units[k]
        copies = []
        for dx in (2, 1, 3):
            dev = (z * 8 + lax.rem(x + dx, 4) * 2 + c, j)
            i = dx - 1
            part = wa.at[pl.ds(1, 3), pl.ds(first, count), row_a]
            copies.append(rem(part, part, wxs.at[2 * k, i], wxr.at[2 * k, i], dev))
            part = wb.at[pl.ds(1, 3), b, row_b]
            copies.append(rem(part, part, wxs.at[2 * k + 1, i], wxr.at[2 * k + 1, i], dev))
        return copies

    def weights_d(k):
        first, count, b = units[k]
        dev = (z * 8 + x * 2 + 1 - c, j)
        part = wa.at[pl.ds(1, 3), pl.ds(first, count), pl.ds(aligned(c * 512, 512), 512)]
        other = wb.at[pl.ds(1, 3), b, pl.ds(aligned(c * 128, 128), 128)]
        return [
            rem(part, part, wds.at[2 * k], wdr.at[2 * k], dev),
            rem(other, other, wds.at[2 * k + 1], wdr.at[2 * k + 1], dev),
        ]

    sent = []

    def start(copies):
        for copy in copies:
            copy.start()
        sent.extend(copies)
        return copies

    def landed(copies):
        for copy in copies:
            copy.wait_recv()

    def send_plane(m, first):
        def step(t, carry):
            halo_copy(m, t).start()
            return carry

        lax.fori_loop(first, 8, step, 0)

    send_plane(0, 1)
    for copy in ld_e:
        copy.wait()
    ey = start(weights_y(0))

    def plane(m, carry):
        pick(m)
        send_plane(m, 0)
        return carry

    lax.fori_loop(1, 8, plane, 0)
    halo_r[0:HALO, :] = picked[pl.ds(aligned((x * 2 + c) * HALO, HALO), HALO), :]

    edges_in = start([
        rem(
            el.at[pl.ds(aligned(pair_of(dy) * ROWS, ROWS), ROWS)], xe.at[:, my_cols],
            es_.at[dy - 1], er_.at[dy - 1], (me, pair_of(dy)),
        )
        for dy in (2, 1, 3)
    ])
    for i, ref in enumerate((eb, eg, es, nb, ng, ns)):
        vec[j, i : i + 1, :] = ref[...]

    vecs = start([
        rem(vec.at[j], vec.at[j], vs.at[dy - 1], vr.at[dy - 1], (me, pair_of(dy)))
        for dy in (2, 1, 3)
    ])

    snd_t = snd[...].T
    rcv_t = rcv[...].T
    lane = iota((TILE, 128), 1)
    for b in range(BLK):
        half = (b % 2) * TILE
        idcol[b // 2, half : half + TILE, :] = snd_t[:, b : b + 1]
        low = ROWS + (b % 2) * HALO
        idcol[b // 2, low : low + HALO, :] = iota((HALO, 1), 0) + own[b] * HALO
        rcol[b] = rcv_t[:, b : b + 1]
        seen = jnp.max(jnp.where(rcv_t[:, b : b + 1] == lane, 1, 0), axis=0, keepdims=True)
        idt[b : b + 1, :] = jnp.where(iota((1, 128), 1) == HALO, own[b], seen)
    low_tri = hot(iota((128, 128), 0) < iota((128, 128), 1))
    live8 = jnp.where(iota((BLK, 128), 1) < HALO, idt[...], 0)
    rank8[...] = jnp.where(live8 > 0, dot(live8.astype(F32).astype(BF), low_tri), -1.0)

    def ids_copy(r):
        return rem(idt, idr.at[me], ids_s, ids_r, (dest(r // 8, lax.rem(r, 8)), j))

    def ids_step(r, carry):
        ids_copy(r).start()
        return carry

    lax.fori_loop(1, PATCH, ids_step, 0)
    idr[me] = idt[...]

    def gather(g):
        slot = g * 16 + iota((1, 512), 1) // HALO
        m = slot // 8
        odd = lax.rem(m, 2)
        dz = odd * ((m + 1) // 2) + (1 - odd) * (8 - m // 2)
        t = lax.rem(slot, 8)
        source = (
            lax.rem(z - dz + 16, 8) * 8 + lax.rem(x - t // 2 + 4, 4) * 2
            + lax.rem(c + lax.rem(t, 2), 2)
        )
        ident = source * HALO + lax.rem(iota((1, 512), 1), HALO)
        low = HALO if g == 0 else 0
        count = 512 - low
        arrived = halo_r.at[pl.ds(g * 512 + low, count)]
        pltpu.make_async_copy(arrived, arrived, hr.at[g]).wait()
        for dy in (2, 1, 3, 0):
            ones = hot(idcol[pair_of(dy)] == ident)
            part = dot(ones, halo_r[g * 512 : (g + 1) * 512, :])
            if g == 0:
                gacc[dy] = part
            elif g < 3:
                gacc[dy] += part
            elif dy == 0:
                xs[:, my_cols] = (gacc[dy] + part).astype(BF)
            else:
                sbuf[dy - 1] = (gacc[dy] + part).astype(BF)
                start([rem(
                    sbuf.at[dy - 1], xs.at[:, my_cols], ss.at[dy - 1], sr.at[dy - 1],
                    (me, pair_of(dy)),
                )])

    gather(0)
    gather(1)
    landed(ey)
    ex = start(weights_x(0))
    gather(2)
    mark = len(sent)
    gather(3)
    rows_in = sent[mark:]

    for copy in ld_x + ld_n:
        copy.wait()
    nodes_in = start([
        rem(
            nl.at[pl.ds(aligned(pair_of(dy) * NROW, NROW), NROW)], xn.at[:, my_cols],
            xns.at[dy - 1], xnr.at[dy - 1], (me, pair_of(dy)),
        )
        for dy in (2, 1, 3)
    ])
    landed(ex)
    ed = start(weights_d(0))

    all_ids = pltpu.make_async_copy(idr.at[pl.ds(0, 63)], idr.at[pl.ds(0, 63)], ids_r)
    all_ids.wait()
    ids = idr[...]
    lane3 = iota((PATCH, BLK, 128), 2)
    holder = jnp.sum(jnp.where(lane3 == HALO, ids, 0), axis=2, keepdims=True)
    seen = jnp.sum(jnp.where((holder == me) & (lane3 < HALO), ids, 0), axis=1)
    seen_f = seen.astype(F32)
    rank = jnp.where(seen > 0, dot(seen_f.astype(BF), low_tri), -1.0)
    listed = jnp.concatenate([hal[0], jnp.zeros((PATCH, 128 - HALO), I32)], axis=1).astype(F32) + 1.0
    wide = iota((PATCH, PATCH * RT), 1)
    mine = wide // RT == iota((PATCH, PATCH * RT), 0)
    spread = jnp.zeros((PATCH, PATCH * RT), F32)
    for r in range(RT):
        node_r = jnp.sum(jnp.where(rank == float(r), listed, 0.0), axis=1, keepdims=True)
        spread = jnp.where(mine & (lax.rem(wide, RT) == r), node_r, spread)
    node_of = jnp.sum(spread, axis=0, keepdims=True).astype(I32) - 1
    amat[...] = hot(iota((NODE, PATCH * RT), 0) == node_of)

    landed(edges_in)
    landed(vecs)
    landed(ed)
    for jr in range(4):
        acc[:, jr * FEAT : (jr + 1) * FEAT] = dot(xe[...], wa[jr, 0]) + vec[pair_of(jr), 0:1, :]
    gain = [jnp.concatenate([vec[k, i : i + 1, :] for k in range(4)], axis=1) for i in (1, 2, 4, 5)]
    landed(rows_in)

    ny = start(weights_y(1))

    def norm(mixed, gain_row, shift_row):
        mean = jnp.sum(mixed, axis=1, keepdims=True) * (1.0 / WIDE)
        spread = jnp.sum(mixed * mixed, axis=1, keepdims=True) * (1.0 / WIDE) - mean * mean
        return (mixed - mean) * lax.rsqrt(spread + EPS) * gain_row + shift_row

    for bb in range(2):
        rows = slice(bb * TILE, (bb + 1) * TILE)
        receiver = rcol[2 * j + bb]
        take = hot(receiver == iota((TILE, HALO), 1))
        mixed = None
        for jr in range(4):
            cols = slice(jr * FEAT, (jr + 1) * FEAT)
            section = dot(xs[ROWS + bb * HALO : ROWS + (bb + 1) * HALO, :], wa[jr, 2]).astype(BF)
            pre = acc[rows, cols] + dot(xs[rows, :], wa[jr, 1]) + dot(take, section)
            hidden = silu(pre).astype(BF)
            term = dot(hidden, wb[jr, 0]).astype(BF).astype(F32)
            mixed = term if mixed is None else mixed + term
        old = xe[rows, :].astype(F32)
        fresh = jnp.where(receiver >= 0, old + norm(mixed, gain[0], gain[1]), old).astype(BF)
        outb[rows, :] = fresh
        rank_row = rank8[pl.ds(2 * j + bb, 1), :][:, 0:HALO]
        which = hot(rank_row == iota((RT, HALO), 0).astype(F32))
        member = hot(rcv[pl.ds(2 * j + bb, 1), :] == iota((HALO, TILE), 0))
        member = dot(which, member).astype(BF)
        tsb[bb * RT : (bb + 1) * RT, :] = dot(member, fresh).astype(BF)

    my_sums = pl.ds(aligned(j * 2 * RT, 2 * RT), 2 * RT)

    def cols_of(dy):
        return pl.ds(aligned(pair_of(dy) * FEAT, FEAT), FEAT)

    sums = start([
        rem(
            tsb.at[:, cols_of(dy)], tsr.at[my_sums], tss.at[dy - 1], tsrr.at[dy - 1],
            (me, pair_of(dy)),
        )
        for dy in (2, 1, 3)
    ])
    tsr[my_sums, :] = tsb[:, my_cols]
    edges_out = start([
        rem(
            outb.at[:, cols_of(dy)], o_e.at[my_edges], oes.at[dy - 1], oer.at[dy - 1],
            (me, pair_of(dy)),
        )
        for dy in (2, 1, 3)
    ])
    keep_e = pltpu.make_async_copy(outb.at[:, my_cols], o_e.at[my_edges], loc.at[10])
    keep_e.start()

    wide_k = iota((1, BLK * RT), 1)
    owner_row = jnp.zeros((1, BLK * RT), I32)
    for b in range(BLK):
        owner_row = jnp.where(wide_k // RT == b, own[b], owner_row)
    rid = iota((PATCH * RT, BLK * RT), 0)
    put = hot((rid // RT == owner_row) & (lax.rem(rid, RT) == lax.rem(wide_k, RT)))
    landed(sums)
    sv[...] = dot(put, tsr[...]).astype(BF)
    my_slot = pl.ds(aligned(me * RT, RT), RT)

    def sum_step(r, carry):
        to = dest(r // 8, lax.rem(r, 8))
        rem(sv.at[pl.ds(aligned(to * RT, RT), RT)], vv.at[my_slot], v2s, v2r, (to, j)).start()
        return carry

    lax.fori_loop(1, PATCH, sum_step, 0)
    vv[my_slot, :] = sv[my_slot, :]

    landed(ny)
    nx = start(weights_x(1))
    landed(nodes_in)
    landed(nx)
    nd = start(weights_d(1))
    landed(nd)
    for jr in range(4):
        acc2[:, jr * FEAT : (jr + 1) * FEAT] = dot(xn[...], wa[jr, 3]) + vec[pair_of(jr), 3:4, :]

    got = vv.at[pl.ds(0, 63 * RT)]
    pltpu.make_async_copy(got, got, v2r).wait()
    mark = len(sent)
    for dy in (2, 1, 3, 0):
        pick_rows = pl.ds(aligned(pair_of(dy) * NROW, NROW), NROW)
        part = dot(amat[pick_rows, :], vv[...]).astype(BF)
        if dy == 0:
            xa[:, my_cols] = part
        else:
            abuf[dy - 1] = part
            start([rem(
                abuf.at[dy - 1], xa.at[:, my_cols], as_.at[dy - 1], ar_.at[dy - 1],
                (me, pair_of(dy)),
            )])
    landed(sent[mark:])
    mixed = None
    for jr in range(4):
        cols = slice(jr * FEAT, (jr + 1) * FEAT)
        hidden = silu(acc2[:, cols] + dot(xa[...], wa[jr, 4])).astype(BF)
        term = dot(hidden, wb[jr, 1]).astype(BF).astype(F32)
        mixed = term if mixed is None else mixed + term
    old = xn[...].astype(F32)
    live = iota((NROW, 1), 0) + j * NROW < cnt[0]
    outn[...] = jnp.where(live, old + norm(mixed, gain[2], gain[3]), old).astype(BF)
    nodes_out = start([
        rem(
            outn.at[:, cols_of(dy)], o_n.at[my_nodes], ons.at[dy - 1], onr.at[dy - 1],
            (me, pair_of(dy)),
        )
        for dy in (2, 1, 3)
    ])
    keep_n = pltpu.make_async_copy(outn.at[:, my_cols], o_n.at[my_nodes], loc.at[11])
    keep_n.start()

    done = picked.at[pl.ds(0, 63 * HALO)]
    pltpu.make_async_copy(done, done, hs).wait()
    pltpu.make_async_copy(idr.at[pl.ds(0, 63)], idr.at[pl.ds(0, 63)], ids_s).wait()
    pltpu.make_async_copy(got, got, v2s).wait()
    for copy in sent:
        copy.wait_send()
    keep_e.wait()
    keep_n.wait()
    landed(edges_out)
    landed(nodes_out)


def shards(
    node_latents, edge_latents, edge_sender, edge_receiver, block_owner, node_counts, halo_nodes,
    w_endpoints, w_edge_in, edge_bias, w_edge_out, edge_gain, edge_shift, w_node_in, node_bias,
    w_node_out, node_gain, node_shift,
):
    row = lambda v: v.reshape(1, FEAT)
    dma = pltpu.SemaphoreType.DMA
    vm = pltpu.VMEM
    scratch = [
        vm((NODE, FEAT), BF), vm((EDGE, 1), I32), vm((EDGE, FEAT), BF), vm((EDGE, FEAT), BF),
        vm((4, SEL, 1), I32), vm((BLK, TILE, 1), I32), vm((BLK, 128), I32), vm((BLK, 128), F32),
        vm((PATCH, BLK, 128), I32), vm((4, 8, FEAT), F32), vm((4, SEL, FEAT), F32),
        vm((3, SEL, FEAT), BF), vm((SEL, WIDE), BF), vm((ROWS, WIDE), BF), vm((NROW, WIDE), BF),
        vm((4, 5, WIDE, FEAT), BF), vm((4, 2, FEAT, WIDE), BF), vm((ROWS, WIDE), F32),
        vm((8, 128), BF), vm((ROWS, WIDE), BF), vm((2 * RT, WIDE), BF), vm((BLK * RT, FEAT), BF),
        vm((PATCH * RT, FEAT), BF), vm((PATCH * RT, FEAT), BF), vm((NODE, PATCH * RT), BF),
        vm((3, NROW, FEAT), BF), vm((NROW, WIDE), BF), vm((NROW, WIDE), F32), vm((NROW, WIDE), BF),
        dma((12,)), dma, dma((4,)), dma, dma, dma((3,)), dma((3,)), dma((3,)), dma((3,)),
        dma((3,)), dma((3,)), dma((4, 3)), dma((4, 3)), dma((4, 3)), dma((4, 3)), dma((4,)),
        dma((4,)), dma((3,)), dma((3,)), dma((3,)), dma((3,)), dma, dma, dma((3,)), dma((3,)),
        dma((3,)), dma((3,)), dma((3,)), dma((3,)),
    ]
    return pl.pallas_call(
        kernel,
        out_shape=(
            jax.ShapeDtypeStruct((NODE, FEAT), BF),
            jax.ShapeDtypeStruct((EDGE, FEAT), BF),
        ),
        in_specs=[ANY, ANY, VM, VM, SM, SM, VM, ANY, ANY, VM, ANY, VM, VM, ANY, VM, ANY, VM, VM],
        out_specs=(ANY, ANY),
        scratch_shapes=scratch,
        compiler_params=pltpu.CompilerParams(
            collective_id=0, has_side_effects=True, vmem_limit_bytes=60 * 2**20
        ),
        name="layer",
    )(
        node_latents, edge_latents, edge_sender, edge_receiver, block_owner, node_counts,
        halo_nodes, jnp.moveaxis(w_endpoints, 1, 0), w_edge_in, row(edge_bias), w_edge_out,
        row(edge_gain), row(edge_shift), w_node_in, row(node_bias), w_node_out, row(node_gain),
        row(node_shift),
    )


def solution(mesh):
    return jax.shard_map(
        shards,
        mesh=mesh,
        in_specs=(
            P("patch", "pair"),
            P("patch", "pair"),
            P("patch", None),
            P("patch", None),
            P("patch"),
            P("patch"),
            P("patch", None, None),
            P(None, None, "pair"),
            P(None, "pair"),
            P("pair"),
            P("pair", None),
            P("pair"),
            P("pair"),
            P(None, None, "pair"),
            P("pair"),
            P("pair", None),
            P("pair"),
            P("pair"),
        ),
        out_specs=(P("patch", "pair"), P("patch", "pair")),
        check_vma=False,
    )
```

time: 380 us -> 158 us (0.42)
  waiting for transfers between devices: 196 us -> 0 us
  Pallas kernels: 0 us -> 150 us
  local copies, waits for them, and re-layouts: 73.2 us -> 6.68 us
  starting transfers between devices: 54.4 us -> 0 us
  matrix products: 21.2 us -> 0 us
  other arithmetic: 17.8 us -> 0 us
  between operations: 15.1 us -> 1.29 us
    all_to_all x8 -> x0, waiting for transfers between devices: 150 us -> none  [the longest x4 62.2 us: copy_for_each(): lax.all_to_all(jnp.broadcast_to(shard[None], (size, *shard.shape)), axis,...]
    pallas_call x0 -> x1, Pallas kernels: none -> 150 us  [shards(): pl.pallas_call(kernel, out_shape=(jax.ShapeDtypeStruct((NODE, FEAT), BF),...]
    gather x4 -> x0, local copies, waits for them, and re-layouts: 57.2 us -> none  [the longest x1 20.5 us: shards(): halo_pairs[edge_owner * halo_size + jnp.maximum(receivers, 0), 1]]
    all_to_all x8 -> x0, starting transfers between devices: 54.3 us -> none  [the longest x1 16.2 us: shards(): lax.all_to_all(picked, 'patch', split_axis=0, concat_axis=0, tiled=True)]
    reduce_scatter x1 -> x0, waiting for transfers between devices: 45.3 us -> none  [shards(): lax.psum_scatter(edge_terms.astype(jnp.bfloat16), 'pair', scatter_dimensi...]
    dot_general x5 -> x0, matrix products: 21.2 us -> none  [the longest x1 9.32 us: shards(): jnp.dot(edge_hidden, w_edge_out, preferred_element_type=jnp.float32)]
    scatter-add x1 -> x0, other arithmetic: 7.79 us -> none  [shards(): jax.ops.segment_sum(got_values.reshape(-1, local_width), node_index.resha...]
    reduce_sum x6 -> x0, other arithmetic: 4.99 us -> none  [the longest x1 2.68 us: shards(): jnp.sum(node_mixed, axis=1)]
  transfers between devices with their start and end apart: 10 -> 0, of which waited for: 9 -> 0; matrix products, arithmetic and copies ran while one was open for 21% -> 0% of each run, Pallas kernels for 0% -> 0%
where the time goes in v1:
time: 158 us
  Pallas kernels  150 us (95%)
  local copies, waits for them, and re-layouts  6.68 us (4%)
    pallas_call x1, Pallas kernels, shards(): pl.pallas_call(kernel, out_shape=(jax.ShapeDtypeStruct((NODE, FEAT), BF),...  150 us
    unnamed x6, local copies, waits for them, and re-layouts  6.68 us

profile of v1, /device:TPU:1, one launch (start us, length us, event | category | flops | bytes accessed | tf_op | source)
XLA Modules:
  0.0 157.8 jit_solution(2183071720132403904)
XLA Ops:
  1.3 1.4 copy.21.hal
  2.7 2.3 %copy.23 = bf16[1024,2,256]{2,0,1:T(8,128)(2,1)} copy(bf16[1024,2,256]{2,1,0:T(2,128)(2,1)} %param.25) | data formatting | bytes 2097152 | tf_op args[7]
  5.0 149.8 %layer.1 = (bf16[1024,256]{1,0:T(8,128)(2,1)}, bf16[2048,256]{1,0:T(8,128)(2,1)}) custom-call(bf16[1024,256]{1,0:T(8,128)(2,1)} %nl.1, bf16[2048,256]{1,0:T(8,128)(2,1)} %el.1, s32[8,256]{1,0:T(8,128)} %snd.1, s32[8,256]{1,0:T(8,128)} %rcv.1, s32[8]{0:T(128)} %own.1, s32[1]{0:T(128)S(6)} %copy.26.cnt, s32[1,64,32]{2,1,0:T(8,128)} %copy.21.hal, ...), custom_call_target="tpu_custom_call" | custom-call | tf_op jit(solution)/shard_map/layer/pallas_call | solution.py:470
  154.8 0.0 copy-start
  154.8 2.0 %copy.27 = bf16[1024,256]{1,0:T(8,128)(2,1)} copy(bf16[1024,256]{1,0:T(8,128)(2,1)} %get-tuple-element.4) | data formatting | bytes 1048576
  156.8 0.0 copy-done
  156.8 1.0 copy.28
Async XLA Ops:
  154.8 2.0 %copy-start = (bf16[2048,256]{1,0:T(8,128)(2,1)S(1)}, bf16[2048,256]{1,0:T(8,128)(2,1)}, u32[]{:S(2)}) copy-start(bf16[2048,256]{1,0:T(8,128)(2,1)} %get-tuple-element.5) | copy-start | bytes 3145732

commit v2 on v1

v2 whole, which is shorter than its diff:
```python
import jax
import jax.numpy as jnp
from jax import lax
from jax.experimental import pallas as pl
from jax.experimental.pallas import tpu as pltpu
from jax.sharding import PartitionSpec as P

EPS = 1e-05
MESH = pl.DeviceIdType.MESH
BF = jnp.bfloat16
F32 = jnp.float32
I32 = jnp.int32

NODE = 1024
EDGE = 2048
FEAT = 256
WIDE = 1024
PATCH = 64
HALO = 32
RT = 16
BLK = 8
TILE = 256
ROWS = 2 * TILE
SEL = ROWS + 2 * HALO
NROW = NODE // 4
PICK = 2
ANY = pl.BlockSpec(memory_space=pl.ANY)
VM = pl.BlockSpec(memory_space=pltpu.VMEM)
SM = pl.BlockSpec(memory_space=pltpu.SMEM)


def iota(shape, dim):
    return lax.broadcasted_iota(I32, shape, dim)


def hot(mask):
    return jnp.where(mask, 1.0, 0.0).astype(BF)


def dot(a, b):
    return jnp.dot(a, b, preferred_element_type=F32)


def silu(v):
    return v / (1.0 + jnp.exp(-v))


def aligned(v, n):
    return pl.multiple_of(v, n)


def kernel(
    nl, el, snd, rcv, own, cnt, hal, wep, win, eb, wout, eg, es, wnin, nb, wnout, ng, ns,
    o_n, o_e,
    nl_v, pcol, picked, halo_r, idcol, rcol, idt, rank8, idr, vec, gacc, sbuf, xs,
    xe, xn, wa, wb, wraw, acc, outb, tsb, tsr, sv, vv, amat, putm, abuf, xa, acc2, outn,
    loc, hs, hr, ids_s, ids_r, es_, er_, xns, xnr, vs, vr,
    wys, wyr, wxs, wxr, wzs, wzr, wds, wdr, ss, sr, tss, tsrr, v2s, v2r, as_, ar_, oes, oer,
    ons, onr,
):
    me = lax.axis_index("patch")
    j = lax.axis_index("pair")
    z, x, c = lax.div(me, 8), lax.rem(lax.div(me, 2), 4), lax.rem(me, 2)
    cell = [
        lax.rem(x + t // 2, 4) * 2 + lax.rem(c + t % 2, 2) for t in range(8)
    ]

    def dz_of(m):
        odd = lax.rem(m, 2)
        return lax.rem(odd * lax.div(m + 1, 2) + (1 - odd) * (8 - lax.div(m, 2)), 8)

    def plane_of(m):
        return lax.rem(z + dz_of(m), 8) * 8

    def rem(src, dst, s, r, dev):
        return pltpu.make_async_remote_copy(
            src_ref=src, dst_ref=dst, send_sem=s, recv_sem=r, device_id=dev, device_id_type=MESH
        )

    def each_patch(act):
        def plane(m, first):
            base = plane_of(m)
            for t in range(first, 8):
                act(m, t, base + cell[t])

        def step(m, carry):
            plane(m, 0)
            return carry

        plane(0, 1)
        lax.fori_loop(1, 8, step, 0)

    pairs = [lax.rem(j + dy, 4) for dy in range(4)]

    scope = []

    def phase(name):
        if scope:
            scope.pop().__exit__(None, None, None)
        if name:
            scope.append(jax.named_scope(name))
            scope[-1].__enter__()

    phase("start")
    loads = []

    def load(src, dst):
        copy = pltpu.make_async_copy(src, dst, loc.at[len(loads)])
        copy.start()
        loads.append(copy)
        return copy

    my_cols = pl.ds(aligned(j * FEAT, FEAT), FEAT)
    my_edges = pl.ds(aligned(j * ROWS, ROWS), ROWS)
    my_nodes = pl.ds(aligned(j * NROW, NROW), NROW)
    ld_nl = load(nl, nl_v)

    barrier = pltpu.get_barrier_semaphore()

    def greet(m, t, to):
        pl.semaphore_signal(barrier, inc=1, device_id=(to, j), device_id_type=MESH)

    for dy in (2, 1, 3):
        pl.semaphore_signal(barrier, inc=1, device_id=(me, pairs[dy]), device_id_type=MESH)
    each_patch(greet)
    ld_e = [load(win, wa.at[0, 0]), load(wep, wraw), load(wout, wb.at[0, 0])]
    ld_x = [load(el.at[my_edges], xe.at[:, my_cols]), load(nl.at[my_nodes], xn.at[:, my_cols])]
    ld_n = [load(wnin.at[0], wa.at[0, 3]), load(wnin.at[1], wa.at[0, 4]), load(wnout, wb.at[0, 1])]

    phase("cols")
    for d in range(PATCH):
        pcol[d * HALO : (d + 1) * HALO, :] = hal[0:HALO, d : d + 1]
    ld_nl.wait()
    phase("pick")

    for m in range(0, 8, PICK):
        wanted = [pcol[pl.ds(aligned(plane_of(m + i) * HALO, 256), 256), :] for i in range(PICK)]
        ones = hot(jnp.concatenate(wanted, axis=0) == iota((PICK * 256, NODE), 1))
        picked[m * 256 : (m + PICK) * 256, :] = dot(ones, nl_v[...]).astype(BF)

    phase("wep")
    piece = c * 4 + x
    for copy in ld_e:
        copy.wait()
    my_rows = pl.ds(aligned(piece * 128, 128), 128)
    wa[0, 1, my_rows, :] = wraw[my_rows, 0, :]
    wa[0, 2, my_rows, :] = wraw[my_rows, 1, :]

    phase("barrier")
    pl.semaphore_wait(barrier, PATCH - 1 + 3)
    phase("sends")

    sent = []

    def start(copies):
        for copy in copies:
            copy.start()
        sent.extend(copies)
        return copies

    def landed(copies):
        for copy in copies:
            copy.wait_recv()

    def seg(u, js, base, low, size):
        if u < 5:
            return wa.at[js, u, pl.ds(aligned(base * 128 + low * 64, 64), size * 64)]
        return wb.at[js, u - 5, pl.ds(aligned(base * 32 + low * 16, 16), size * 16)]

    others = pl.ds(1, 3)

    def weights_y(u):
        return start([
            rem(
                seg(u, 0, piece, 0, 2), seg(u, 4 - dy, piece, 0, 2),
                wys.at[u, dy - 1], wyr.at[u, dy - 1], (me, pairs[dy]),
            )
            for dy in (2, 1, 3)
        ])

    right = z * 8 + lax.rem(x + 1, 4) * 2 + c
    left = z * 8 + lax.rem(x + 3, 4) * 2 + c

    def weights_x(u):
        part = seg(u, others, piece, 0, 2)
        return start([
            rem(part, part, wxs.at[u, i], wxr.at[u, i], (to, j)) for i, to in ((0, right), (1, left))
        ])

    def weights_z(u):
        from_left = seg(u, others, c * 4 + lax.rem(x + 3, 4), 0, 1)
        from_right = seg(u, others, c * 4 + lax.rem(x + 1, 4), 1, 1)
        return start([
            rem(from_left, from_left, wzs.at[u, 0], wzr.at[u, 0], (right, j)),
            rem(from_right, from_right, wzs.at[u, 1], wzr.at[u, 1], (left, j)),
        ])

    def weights_d(u):
        part = seg(u, others, c * 4, 0, 8)
        return start([rem(part, part, wds.at[u], wdr.at[u], (z * 8 + x * 2 + 1 - c, j))])

    def send_halo(m, t, to):
        rem(
            picked.at[pl.ds(aligned(m * 256 + cell[t] * HALO, HALO), HALO)],
            halo_r.at[pl.ds(aligned((m * 8 + t) * HALO, HALO), HALO)],
            hs, hr.at[lax.div(m, 2)], (to, j),
        ).start()

    order_e = (0, 1, 2, 5)
    wy = {u: weights_y(u) for u in order_e}
    each_patch(send_halo)
    halo_r[0:HALO, :] = picked[pl.ds(aligned(cell[0] * HALO, HALO), HALO), :]
    part_a, part_b = slice(0, TILE + 2 * HALO), slice(TILE + 2 * HALO, SEL)

    def gather(g):
        slot = g * 16 + iota((1, 512), 1) // HALO
        m = slot // 8
        odd = lax.rem(m, 2)
        dz = odd * ((m + 1) // 2) + (1 - odd) * (8 - m // 2)
        t = lax.rem(slot, 8)
        source = (
            lax.rem(z - dz + 16, 8) * 8 + lax.rem(x - t // 2 + 4, 4) * 2
            + lax.rem(c + lax.rem(t, 2), 2)
        )
        ident = source * HALO + lax.rem(iota((1, 512), 1), HALO)
        low = HALO if g == 0 else 0
        arrived = halo_r.at[pl.ds(g * 512 + low, 512 - low)]
        pltpu.make_async_copy(arrived, arrived, hr.at[g]).wait()
        table = halo_r.at[g * 512 : (g + 1) * 512]
        if g < 3:
            for dy in (2, 1, 3, 0):
                part = dot(hot(idcol[pairs[dy]] == ident), table[...])
                gacc[dy] = part if g == 0 else gacc[dy] + part
            return []
        copies = []
        for half, rows in enumerate((part_a, part_b)):
            for dy in (2, 1, 3, 0):
                part = dot(hot(idcol[pairs[dy], rows, :] == ident), table[...])
                part = (gacc[dy, rows, :] + part).astype(BF)
                if dy == 0:
                    xs[rows, my_cols] = part
                else:
                    sbuf[dy - 1, rows, :] = part
                    copies.append(rem(
                        sbuf.at[dy - 1, rows], xs.at[rows, my_cols], ss.at[half, dy - 1],
                        sr.at[half, dy - 1], (me, pairs[dy]),
                    ))
                    start(copies[-1:])
        return copies

    wx, wz, wd = {}, {}, {}

    def wy_to_x(u):
        landed(wy[u])
        wx[u] = weights_x(u)

    def x_to_z(u):
        landed(wx[u])
        wz[u] = weights_z(u)

    def z_to_d(u):
        landed(wz[u])
        wd[u] = weights_d(u)

    def block_ids():
        snd_t = snd[...].T
        rcv_t = rcv[...].T
        lane = iota((TILE, 128), 1)
        for b in range(BLK):
            g, low = b // 2, (b % 2) * (TILE + 2 * HALO)
            idcol[g, low : low + TILE, :] = snd_t[:, b : b + 1]
            low = TILE + (b % 2) * HALO
            idcol[g, low : low + HALO, :] = iota((HALO, 1), 0) + own[b] * HALO
            rcol[b] = rcv_t[:, b : b + 1]
            seen = jnp.max(jnp.where(rcv_t[:, b : b + 1] == lane, 1, 0), axis=0, keepdims=True)
            idt[b : b + 1, :] = jnp.where(iota((1, 128), 1) == HALO, own[b], seen)

    phase("idcols")
    block_ids()
    for i, ref in enumerate((eb, eg, es, nb, ng, ns)):
        vec[j, i : i + 1, :] = ref[...]
    phase("vecs")
    vecs = start([
        rem(vec.at[j], vec.at[j], vs.at[dy - 1], vr.at[dy - 1], (me, pairs[dy]))
        for dy in (2, 1, 3)
    ])

    phase("wy0")
    wy_to_x(0)
    phase("wep2")

    def split(k, carry):
        rows = pl.ds(aligned(lax.rem(piece + k, 8) * 128, 128), 128)
        wa[0, 1, rows, :] = wraw[rows, 0, :]
        wa[0, 2, rows, :] = wraw[rows, 1, :]
        return carry

    lax.fori_loop(1, 8, split, 0)
    phase("g0")
    gather(0)
    phase("wy1")
    wy_to_x(1)
    phase("wy2")
    wy_to_x(2)
    phase("g1")
    gather(1)
    phase("wy5")
    wy_to_x(5)
    phase("edgesin")
    edges_in = start([
        rem(
            el.at[pl.ds(aligned(pairs[dy] * ROWS, ROWS), ROWS)], xe.at[:, my_cols],
            es_.at[dy - 1], er_.at[dy - 1], (me, pairs[dy]),
        )
        for dy in (2, 1, 3)
    ])
    phase("x0")
    x_to_z(0)
    phase("g2")
    gather(2)
    phase("ny")
    for copy in ld_n:
        copy.wait()
    for u in (3, 4):
        wy[u] = weights_y(u)
    phase("x1")
    x_to_z(1)
    phase("g3")
    rows_in = gather(3)
    phase("ldn")
    for copy in ld_x:
        copy.wait()
    def send_ids(m, t, to):
        rem(idt, idr.at[me], ids_s, ids_r, (to, j)).start()

    each_patch(send_ids)
    idr[me] = idt[...]

    phase("z0")
    z_to_d(0)
    phase("x2")
    x_to_z(2)
    phase("z1")
    z_to_d(1)

    phase("tables")
    low_tri = hot(iota((128, 128), 0) < iota((128, 128), 1))
    live8 = jnp.where(iota((BLK, 128), 1) < HALO, idt[...], 0)
    rank8[...] = jnp.where(live8 > 0, dot(live8.astype(F32).astype(BF), low_tri), -1.0)
    all_ids = pltpu.make_async_copy(idr.at[pl.ds(0, 63)], idr.at[pl.ds(0, 63)], ids_r)
    all_ids.wait()
    ids = idr[...]
    lane3 = iota((PATCH, BLK, 128), 2)
    holder = jnp.sum(jnp.where(lane3 == HALO, ids, 0), axis=2, keepdims=True)
    seen = jnp.sum(jnp.where((holder == me) & (lane3 < HALO), ids, 0), axis=1)
    rank = jnp.where(seen > 0, dot(seen.astype(F32).astype(BF), low_tri), -1.0)
    listed = jnp.concatenate([hal[...], jnp.zeros((HALO, PATCH), I32)], axis=1)
    listed = jnp.concatenate([listed, jnp.zeros((128 - HALO, 128), I32)], axis=0)
    listed = listed.T[0:PATCH].astype(F32) + 1.0
    wide = iota((PATCH, PATCH * RT), 1)
    mine = wide // RT == iota((PATCH, PATCH * RT), 0)
    spread = jnp.zeros((PATCH, PATCH * RT), F32)
    for r in range(RT):
        node_r = jnp.sum(jnp.where(rank == float(r), listed, 0.0), axis=1, keepdims=True)
        spread = jnp.where(mine & (lax.rem(wide, RT) == r), node_r, spread)
    node_of = jnp.sum(spread, axis=0, keepdims=True).astype(I32) - 1
    amat[...] = hot(iota((NODE, PATCH * RT), 0) == node_of)
    wide_k = iota((1, BLK * RT), 1)
    owner_row = jnp.zeros((1, BLK * RT), I32)
    for b in range(BLK):
        owner_row = jnp.where(wide_k // RT == b, own[b], owner_row)
    rid = iota((PATCH * RT, BLK * RT), 0)
    putm[...] = hot((rid // RT == owner_row) & (lax.rem(rid, RT) == lax.rem(wide_k, RT)))

    phase("x5")
    x_to_z(5)
    phase("z2")
    z_to_d(2)
    phase("w_edges")
    landed(edges_in)
    landed(vecs)
    phase("w_d0")
    landed(wd[0])
    phase("edge1")
    for jr in range(4):
        acc[:, jr * FEAT : (jr + 1) * FEAT] = dot(xe[...], wa[jr, 0]) + vec[pairs[jr], 0:1, :]
    gain = [jnp.concatenate([vec[k, i : i + 1, :] for k in range(4)], axis=1) for i in (1, 2, 4, 5)]
    phase("z5")
    z_to_d(5)
    phase("n34")
    wy_to_x(3)
    wy_to_x(4)
    phase("w_rows0")
    landed(rows_in[0:3])
    wy[6] = weights_y(6)
    phase("w_d")
    landed(wd[1])
    landed(wd[2])
    landed(wd[5])

    def norm(mixed, gain_row, shift_row):
        mean = jnp.sum(mixed, axis=1, keepdims=True) * (1.0 / WIDE)
        spread = jnp.sum(mixed * mixed, axis=1, keepdims=True) * (1.0 / WIDE) - mean * mean
        return (mixed - mean) * lax.rsqrt(spread + EPS) * gain_row + shift_row

    section = [dot(xs[TILE : TILE + 2 * HALO, :], wa[k, 2]).astype(BF) for k in range(4)]
    for bb in range(2):
        if bb:
            phase("w_rows1")
            landed(rows_in[3:6])
        phase("edge2_%d" % bb)
        rows = slice(bb * TILE, (bb + 1) * TILE)
        in_xs = slice(bb * (TILE + 2 * HALO), bb * (TILE + 2 * HALO) + TILE)
        receiver = rcol[2 * j + bb]
        take = hot(receiver == iota((TILE, HALO), 1))
        mixed = None
        for jr in range(4):
            cols = slice(jr * FEAT, (jr + 1) * FEAT)
            pre = acc[rows, cols] + dot(xs[in_xs, :], wa[jr, 1])
            pre = pre + dot(take, section[jr][bb * HALO : (bb + 1) * HALO, :])
            hidden = silu(pre).astype(BF)
            term = dot(hidden, wb[jr, 0]).astype(BF).astype(F32)
            mixed = term if mixed is None else mixed + term
        old = xe[rows, :].astype(F32)
        fresh = jnp.where(receiver >= 0, old + norm(mixed, gain[0], gain[1]), old).astype(BF)
        outb[rows, :] = fresh
        rank_row = rank8[pl.ds(2 * j + bb, 1), :][:, 0:HALO]
        which = hot(rank_row == iota((RT, HALO), 0).astype(F32))
        member = hot(rcv[pl.ds(2 * j + bb, 1), :] == iota((HALO, TILE), 0))
        member = dot(which, member).astype(BF)
        tsb[bb * RT : (bb + 1) * RT, :] = dot(member, fresh).astype(BF)

    phase("esend")
    my_sums = pl.ds(aligned(j * 2 * RT, 2 * RT), 2 * RT)

    def cols_of(dy):
        return pl.ds(aligned(pairs[dy] * FEAT, FEAT), FEAT)

    sums = start([
        rem(
            tsb.at[:, cols_of(dy)], tsr.at[my_sums], tss.at[dy - 1], tsrr.at[dy - 1],
            (me, pairs[dy]),
        )
        for dy in (2, 1, 3)
    ])
    tsr[my_sums, :] = tsb[:, my_cols]
    phase("w_sums")
    landed(sums)
    phase("sumsend")
    sv[...] = dot(putm[...], tsr[...]).astype(BF)
    my_slot = pl.ds(aligned(me * RT, RT), RT)

    def send_sum(m, t, to):
        rem(sv.at[pl.ds(aligned(to * RT, RT), RT)], vv.at[my_slot], v2s, v2r, (to, j)).start()

    each_patch(send_sum)
    vv[my_slot, :] = sv[my_slot, :]

    phase("eout")
    nodes_in = start([
        rem(
            nl.at[pl.ds(aligned(pairs[dy] * NROW, NROW), NROW)], xn.at[:, my_cols],
            xns.at[dy - 1], xnr.at[dy - 1], (me, pairs[dy]),
        )
        for dy in (2, 1, 3)
    ])
    edges_out = start([
        rem(
            outb.at[:, cols_of(dy)], o_e.at[my_edges], oes.at[dy - 1], oer.at[dy - 1],
            (me, pairs[dy]),
        )
        for dy in (2, 1, 3)
    ])
    keep_e = pltpu.make_async_copy(outb.at[:, my_cols], o_e.at[my_edges], loc.at[10])
    keep_e.start()

    phase("w_ny")
    wy_to_x(6)
    phase("w_nx")
    for u in (3, 4, 6):
        x_to_z(u)
    phase("w_nz")
    for u in (3, 4, 6):
        z_to_d(u)
    phase("w_nin")
    landed(nodes_in)
    phase("w_nd")
    for u in (3, 4, 6):
        landed(wd[u])
    phase("node1")
    for jr in range(4):
        acc2[:, jr * FEAT : (jr + 1) * FEAT] = dot(xn[...], wa[jr, 3]) + vec[pairs[jr], 3:4, :]

    phase("w_vv")
    got = vv.at[pl.ds(0, 63 * RT)]
    pltpu.make_async_copy(got, got, v2r).wait()
    phase("agg")
    half_n = NROW // 2
    agg_in = []
    for h in range(2):
        rows = slice(h * half_n, (h + 1) * half_n)
        for dy in (2, 1, 3, 0):
            from_rows = pl.ds(aligned(pairs[dy] * NROW + h * half_n, half_n), half_n)
            part = dot(amat[from_rows, :], vv[...]).astype(BF)
            if dy == 0:
                xa[rows, my_cols] = part
            else:
                abuf[dy - 1, rows, :] = part
                agg_in.append(rem(
                    abuf.at[dy - 1, rows], xa.at[rows, my_cols], as_.at[h, dy - 1],
                    ar_.at[h, dy - 1], (me, pairs[dy]),
                ))
                start(agg_in[-1:])
    nodes_out = []
    keep_n = []
    for h in range(2):
        phase("w_agg%d" % h)
        landed(agg_in[3 * h : 3 * h + 3])
        phase("node2_%d" % h)
        rows = slice(h * half_n, (h + 1) * half_n)
        mixed = None
        for jr in range(4):
            cols = slice(jr * FEAT, (jr + 1) * FEAT)
            hidden = silu(acc2[rows, cols] + dot(xa[rows, :], wa[jr, 4])).astype(BF)
            term = dot(hidden, wb[jr, 1]).astype(BF).astype(F32)
            mixed = term if mixed is None else mixed + term
        old = xn[rows, :].astype(F32)
        live = iota((half_n, 1), 0) + (j * NROW + h * half_n) < cnt[0]
        outn[rows, :] = jnp.where(live, old + norm(mixed, gain[2], gain[3]), old).astype(BF)
        to_rows = pl.ds(aligned(j * NROW + h * half_n, half_n), half_n)
        nodes_out.extend(start([
            rem(
                outn.at[rows, cols_of(dy)], o_n.at[to_rows], ons.at[h, dy - 1], onr.at[h, dy - 1],
                (me, pairs[dy]),
            )
            for dy in (2, 1, 3)
        ]))
        copy = pltpu.make_async_copy(outn.at[rows, my_cols], o_n.at[to_rows], loc.at[11 + h])
        copy.start()
        keep_n.append(copy)

    phase("end_s")
    done = picked.at[pl.ds(0, 63 * HALO)]
    pltpu.make_async_copy(done, done, hs).wait()
    pltpu.make_async_copy(idr.at[pl.ds(0, 63)], idr.at[pl.ds(0, 63)], ids_s).wait()
    pltpu.make_async_copy(got, got, v2s).wait()
    for copy in sent:
        copy.wait_send()
    keep_e.wait()
    for copy in keep_n:
        copy.wait()
    phase("end_e")
    landed(edges_out)
    phase("end_n")
    landed(nodes_out)
    phase(None)


def shards(
    node_latents, edge_latents, edge_sender, edge_receiver, block_owner, node_counts, halo_nodes,
    w_endpoints, w_edge_in, edge_bias, w_edge_out, edge_gain, edge_shift, w_node_in, node_bias,
    w_node_out, node_gain, node_shift,
):
    row = lambda v: v.reshape(1, FEAT)
    dma = pltpu.SemaphoreType.DMA
    vm = pltpu.VMEM
    scratch = [
        vm((NODE, FEAT), BF), vm((EDGE, 1), I32), vm((EDGE, FEAT), BF), vm((EDGE, FEAT), BF),
        vm((4, SEL, 1), I32), vm((BLK, TILE, 1), I32), vm((BLK, 128), I32), vm((BLK, 128), F32),
        vm((PATCH, BLK, 128), I32), vm((4, 8, FEAT), F32), vm((4, SEL, FEAT), F32),
        vm((3, SEL, FEAT), BF), vm((SEL, WIDE), BF), vm((ROWS, WIDE), BF), vm((NROW, WIDE), BF),
        vm((4, 5, WIDE, FEAT), BF), vm((4, 2, FEAT, WIDE), BF), vm((WIDE, 2, FEAT), BF),
        vm((ROWS, WIDE), F32), vm((ROWS, WIDE), BF), vm((2 * RT, WIDE), BF),
        vm((BLK * RT, FEAT), BF), vm((PATCH * RT, FEAT), BF), vm((PATCH * RT, FEAT), BF),
        vm((NODE, PATCH * RT), BF), vm((PATCH * RT, BLK * RT), BF), vm((3, NROW, FEAT), BF),
        vm((NROW, WIDE), BF), vm((NROW, WIDE), F32), vm((NROW, WIDE), BF),
        dma((13,)), dma, dma((4,)), dma, dma, dma((3,)), dma((3,)), dma((3,)), dma((3,)),
        dma((3,)), dma((3,)), dma((7, 3)), dma((7, 3)), dma((7, 2)), dma((7, 2)), dma((7, 2)),
        dma((7, 2)), dma((7,)), dma((7,)), dma((2, 3)), dma((2, 3)), dma((3,)), dma((3,)), dma,
        dma, dma((2, 3)), dma((2, 3)), dma((3,)), dma((3,)), dma((2, 3)), dma((2, 3)),
    ]
    return pl.pallas_call(
        kernel,
        out_shape=(
            jax.ShapeDtypeStruct((NODE, FEAT), BF),
            jax.ShapeDtypeStruct((EDGE, FEAT), BF),
        ),
        in_specs=[ANY, ANY, VM, VM, SM, SM, VM, ANY, ANY, VM, ANY, VM, VM, ANY, VM, ANY, VM, VM],
        out_specs=(ANY, ANY),
        scratch_shapes=scratch,
        compiler_params=pltpu.CompilerParams(
            collective_id=0, has_side_effects=True, vmem_limit_bytes=60 * 2**20
        ),
        name="layer",
    )(
        node_latents, edge_latents, edge_sender, edge_receiver, block_owner, node_counts,
        halo_nodes[0].T, w_endpoints, w_edge_in, row(edge_bias), w_edge_out,
        row(edge_gain), row(edge_shift), w_node_in, row(node_bias), w_node_out, row(node_gain),
        row(node_shift),
    )


def solution(mesh):
    return jax.shard_map(
        shards,
        mesh=mesh,
        in_specs=(
            P("patch", "pair"),
            P("patch", "pair"),
            P("patch", None),
            P("patch", None),
            P("patch"),
            P("patch"),
            P("patch", None, None),
            P(None, None, "pair"),
            P(None, "pair"),
            P("pair"),
            P("pair", None),
            P("pair"),
            P("pair"),
            P(None, None, "pair"),
            P("pair"),
            P("pair", None),
            P("pair"),
            P("pair"),
        ),
        out_specs=(P("patch", "pair"), P("patch", "pair")),
        check_vma=False,
    )
```

time: 158 us -> 114 us (0.72)
  Pallas kernels: 150 us -> 110 us
  local copies, waits for them, and re-layouts: 6.68 us -> 2.93 us
    pallas_call x1, Pallas kernels: 150 us -> 110 us  [shards(): pl.pallas_call(kernel, out_shape=(jax.ShapeDtypeStruct((NODE, FEAT), BF),...]
    unnamed x6 -> x4, local copies, waits for them, and re-layouts: 6.68 us -> 2.93 us
where the time goes in v2:
time: 114 us
  Pallas kernels  110 us (96%)
  local copies, waits for them, and re-layouts  2.93 us (3%)
  between operations  1.3 us (1%)
    pallas_call x1, Pallas kernels, shards(): pl.pallas_call(kernel, out_shape=(jax.ShapeDtypeStruct((NODE, FEAT), BF),...  110 us
    unnamed x4, local copies, waits for them, and re-layouts  2.93 us

profile of v2, /device:TPU:1, one launch (start us, length us, event | category | flops | bytes accessed | tf_op | source)
XLA Modules:
  0.0 113.7 jit_solution(13227064165216854608)
XLA Ops:
  1.3 109.5 %layer.1 = (bf16[1024,256]{1,0:T(8,128)(2,1)}, bf16[2048,256]{1,0:T(8,128)(2,1)}) custom-call(bf16[1024,256]{1,0:T(8,128)(2,1)} %nl.1, bf16[2048,256]{1,0:T(8,128)(2,1)} %el.1, s32[8,256]{1,0:T(8,128)} %snd.1, s32[8,256]{1,0:T(8,128)} %rcv.1, s32[8]{0:T(128)} %own.1, s32[1]{0:T(128)S(6)} %copy.22.cnt, s32[32,64]{1,0:T(8,128)} %bitcast.9, ...), custom_call_target="tpu_custom_call" | custom-call | tf_op jit(solution)/shard_map/layer/pallas_call | solution.py:582
  110.8 0.0 copy-start
  110.8 2.0 %copy.23 = bf16[1024,256]{1,0:T(8,128)(2,1)} copy(bf16[1024,256]{1,0:T(8,128)(2,1)} %get-tuple-element.4) | data formatting | bytes 1048576
  112.8 0.0 copy-done
  112.8 1.0 copy.24
Async XLA Ops:
  110.8 2.0 %copy-start = (bf16[2048,256]{1,0:T(8,128)(2,1)S(1)}, bf16[2048,256]{1,0:T(8,128)(2,1)}, u32[]{:S(2)}) copy-start(bf16[2048,256]{1,0:T(8,128)(2,1)} %get-tuple-element.5) | copy-start | bytes 3145732

commit v3 on v2

--- a/solution.py
+++ b/solution.py
@@ -24,9 +24,9 @@
 SEL = ROWS + 2 * HALO
 NROW = NODE // 4
 PICK = 2
+CUT = 512
 ANY = pl.BlockSpec(memory_space=pl.ANY)
 VM = pl.BlockSpec(memory_space=pltpu.VMEM)
-SM = pl.BlockSpec(memory_space=pltpu.SMEM)
 
 
 def iota(shape, dim):
@@ -50,12 +50,12 @@
 
 
 def kernel(
-    nl, el, snd, rcv, own, cnt, hal, wep, win, eb, wout, eg, es, wnin, nb, wnout, ng, ns,
+    nl, el, snd_h, rcv_h, own_h, cnt_h, hal_h, wep, win, eb, wout, eg, es, wnin, nb, wnout, ng, ns,
     o_n, o_e,
-    nl_v, pcol, picked, halo_r, idcol, rcol, idt, rank8, idr, vec, gacc, sbuf, xs,
-    xe, xn, wa, wb, wraw, acc, outb, tsb, tsr, sv, vv, amat, putm, abuf, xa, acc2, outn,
+    own, cnt, snd, rcv, hal, nl_v, pcol, picked, halo_r, idcol, rcol, idt, idm, rank8, idr, vec, gacc, sbuf, xs,
+    xe, xn, wa, wb, wraw, acc, hid, outb, tsb, tsr, sv, vv, amat, putm, abuf, xa, acc2, outn,
     loc, hs, hr, ids_s, ids_r, es_, er_, xns, xnr, vs, vr,
-    wys, wyr, wxs, wxr, wzs, wzr, wds, wdr, ss, sr, tss, tsrr, v2s, v2r, as_, ar_, oes, oer,
+    wys, wyr, wxs, wxr, wzs, wzr, wrs, wrr, wds, wdr, ss, sr, tss, tsrr, v2s, v2r, as_, ar_, oes, oer,
     ons, onr,
 ):
     me = lax.axis_index("patch")
@@ -113,6 +113,7 @@
     my_cols = pl.ds(aligned(j * FEAT, FEAT), FEAT)
     my_edges = pl.ds(aligned(j * ROWS, ROWS), ROWS)
     my_nodes = pl.ds(aligned(j * NROW, NROW), NROW)
+    ld_hal = load(hal_h, hal)
     ld_nl = load(nl, nl_v)
 
     barrier = pltpu.get_barrier_semaphore()
@@ -120,14 +121,27 @@
     def greet(m, t, to):
         pl.semaphore_signal(barrier, inc=1, device_id=(to, j), device_id_type=MESH)
 
+    def greet_plane(m, carry):
+        base = plane_of(7 - m)
+        for t in range(8):
+            greet(7 - m, t, base + cell[t])
+        return carry
+
     for dy in (2, 1, 3):
         pl.semaphore_signal(barrier, inc=1, device_id=(me, pairs[dy]), device_id_type=MESH)
-    each_patch(greet)
+    lax.fori_loop(0, 7, greet_plane, 0)
+    for t in range(1, 8):
+        greet(0, t, plane_of(0) + cell[t])
     ld_e = [load(win, wa.at[0, 0]), load(wep, wraw), load(wout, wb.at[0, 0])]
+    ld_i = [load(snd_h, snd), load(rcv_h, rcv), load(own_h, own), load(cnt_h, cnt)]
+    ld_i += [
+        load(ref, vec.at[j, pl.ds(i, 1)]) for i, ref in enumerate((eb, eg, es, nb, ng, ns))
+    ]
     ld_x = [load(el.at[my_edges], xe.at[:, my_cols]), load(nl.at[my_nodes], xn.at[:, my_cols])]
     ld_n = [load(wnin.at[0], wa.at[0, 3]), load(wnin.at[1], wa.at[0, 4]), load(wnout, wb.at[0, 1])]
 
     phase("cols")
+    ld_hal.wait()
     for d in range(PATCH):
         pcol[d * HALO : (d + 1) * HALO, :] = hal[0:HALO, d : d + 1]
     ld_nl.wait()
@@ -165,14 +179,21 @@
     def seg(u, js, base, low, size):
         if u < 5:
             return wa.at[js, u, pl.ds(aligned(base * 128 + low * 64, 64), size * 64)]
-        return wb.at[js, u - 5, pl.ds(aligned(base * 32 + low * 16, 16), size * 16)]
+        rows = pl.ds(aligned(base * 32 + low * 16, 16), size * 16)
+        cols = pl.ds(0, CUT) if u < 7 else pl.ds(CUT, WIDE - CUT)
+        return wb.at[js, (u + 1) % 2, rows, cols]
+
+    def thin(u, js):
+        rows = pl.ds(aligned((c * 8 + z) * 16, 16), 16)
+        return wb.at[js, (u + 1) % 2, rows, pl.ds(0, CUT)]
 
     others = pl.ds(1, 3)
 
     def weights_y(u):
         return start([
             rem(
-                seg(u, 0, piece, 0, 2), seg(u, 4 - dy, piece, 0, 2),
+                thin(u, 0) if u in (5, 6) else seg(u, 0, piece, 0, 2),
+                thin(u, 4 - dy) if u in (5, 6) else seg(u, 4 - dy, piece, 0, 2),
                 wys.at[u, dy - 1], wyr.at[u, dy - 1], (me, pairs[dy]),
             )
             for dy in (2, 1, 3)
@@ -195,6 +216,15 @@
             rem(from_right, from_right, wzs.at[u, 1], wzr.at[u, 1], (left, j)),
         ])
 
+    def weights_round(u):
+        return start([
+            rem(
+                thin(u, others), thin(u, others), wrs.at[u - 5, dz - 1], wrr.at[u - 5, dz - 1],
+                (lax.rem(z + dz, 8) * 8 + x * 2 + c, j),
+            )
+            for dz in (4, 3, 5, 2, 6, 1, 7)
+        ])
+
     def weights_d(u):
         part = seg(u, others, c * 4, 0, 8)
         return start([rem(part, part, wds.at[u], wdr.at[u], (z * 8 + x * 2 + 1 - c, j))])
@@ -206,10 +236,12 @@
             hs, hr.at[lax.div(m, 2)], (to, j),
         ).start()
 
-    order_e = (0, 1, 2, 5)
-    wy = {u: weights_y(u) for u in order_e}
+    order_e = (0, 1, 2, 7, 5)
+    wy = {0: weights_y(0)}
     each_patch(send_halo)
     halo_r[0:HALO, :] = picked[pl.ds(aligned(cell[0] * HALO, HALO), HALO), :]
+    wx, wz, wd = {}, {}, {}
+
     part_a, part_b = slice(0, TILE + 2 * HALO), slice(TILE + 2 * HALO, SEL)
 
     def gather(g):
@@ -226,6 +258,8 @@
         low = HALO if g == 0 else 0
         arrived = halo_r.at[pl.ds(g * 512 + low, 512 - low)]
         pltpu.make_async_copy(arrived, arrived, hr.at[g]).wait()
+        if g == 3:
+            wz[5] = weights_round(5)
         table = halo_r.at[g * 512 : (g + 1) * 512]
         if g < 3:
             for dy in (2, 1, 3, 0):
@@ -248,8 +282,6 @@
                     start(copies[-1:])
         return copies
 
-    wx, wz, wd = {}, {}, {}
-
     def wy_to_x(u):
         landed(wy[u])
         wx[u] = weights_x(u)
@@ -267,19 +299,21 @@
         rcv_t = rcv[...].T
         lane = iota((TILE, 128), 1)
         for b in range(BLK):
-            g, low = b // 2, (b % 2) * (TILE + 2 * HALO)
+            g, low = b // 2, 2 * HALO + (b % 2) * TILE
             idcol[g, low : low + TILE, :] = snd_t[:, b : b + 1]
-            low = TILE + (b % 2) * HALO
+            low = (b % 2) * HALO
             idcol[g, low : low + HALO, :] = iota((HALO, 1), 0) + own[b] * HALO
             rcol[b] = rcv_t[:, b : b + 1]
             seen = jnp.max(jnp.where(rcv_t[:, b : b + 1] == lane, 1, 0), axis=0, keepdims=True)
-            idt[b : b + 1, :] = jnp.where(iota((1, 128), 1) == HALO, own[b], seen)
+            idt[b : b + 1, :] = seen
 
     phase("idcols")
+    for copy in ld_i:
+        copy.wait()
     block_ids()
-    for i, ref in enumerate((eb, eg, es, nb, ng, ns)):
-        vec[j, i : i + 1, :] = ref[...]
     phase("vecs")
+    for u in order_e[1:]:
+        wy[u] = weights_y(u)
     vecs = start([
         rem(vec.at[j], vec.at[j], vs.at[dy - 1], vr.at[dy - 1], (me, pairs[dy]))
         for dy in (2, 1, 3)
@@ -296,16 +330,6 @@
         return carry
 
     lax.fori_loop(1, 8, split, 0)
-    phase("g0")
-    gather(0)
-    phase("wy1")
-    wy_to_x(1)
-    phase("wy2")
-    wy_to_x(2)
-    phase("g1")
-    gather(1)
-    phase("wy5")
-    wy_to_x(5)
     phase("edgesin")
     edges_in = start([
         rem(
@@ -314,15 +338,26 @@
         )
         for dy in (2, 1, 3)
     ])
+    phase("g0")
+    gather(0)
+    phase("wy1")
+    wy_to_x(1)
+    phase("wy2")
+    wy_to_x(2)
+    for copy in ld_n:
+        copy.wait()
+    for u in (3, 6):
+        wy[u] = weights_y(u)
+    phase("g1")
+    gather(1)
+    phase("wy5")
+    landed(wy[5])
+    wy_to_x(7)
     phase("x0")
     x_to_z(0)
     phase("g2")
     gather(2)
     phase("ny")
-    for copy in ld_n:
-        copy.wait()
-    for u in (3, 4):
-        wy[u] = weights_y(u)
     phase("x1")
     x_to_z(1)
     phase("g3")
@@ -330,41 +365,37 @@
     phase("ldn")
     for copy in ld_x:
         copy.wait()
-    def send_ids(m, t, to):
-        rem(idt, idr.at[me], ids_s, ids_r, (to, j)).start()
-
-    each_patch(send_ids)
-    idr[me] = idt[...]
-
     phase("z0")
     z_to_d(0)
     phase("x2")
     x_to_z(2)
+    phase("x7")
+    x_to_z(7)
     phase("z1")
     z_to_d(1)
 
     phase("tables")
     low_tri = hot(iota((128, 128), 0) < iota((128, 128), 1))
     live8 = jnp.where(iota((BLK, 128), 1) < HALO, idt[...], 0)
+    lane8 = iota((BLK, 128), 1)
+    bit = lax.shift_left(jnp.ones((BLK, 128), I32), lax.rem(lane8, 16))
+    bits = [
+        jnp.sum(jnp.where(lane8 // 16 == k, live8 * bit, 0), axis=1, keepdims=True) for k in range(2)
+    ]
+    lane1 = iota((1, 128), 1)
+    message = jnp.zeros((1, 128), I32)
+    for b in range(BLK):
+        message = jnp.where(lane1 == b * 16, own[b], message)
+        for k in range(2):
+            message = jnp.where(lane1 == b * 16 + 1 + k, bits[k][b : b + 1, :], message)
+    idm[...] = message
+    def send_ids(m, t, to):
+        rem(idm, idr.at[me], ids_s, ids_r, (to, j)).start()
+
+    each_patch(send_ids)
+    idr[me] = idm[...]
+
     rank8[...] = jnp.where(live8 > 0, dot(live8.astype(F32).astype(BF), low_tri), -1.0)
-    all_ids = pltpu.make_async_copy(idr.at[pl.ds(0, 63)], idr.at[pl.ds(0, 63)], ids_r)
-    all_ids.wait()
-    ids = idr[...]
-    lane3 = iota((PATCH, BLK, 128), 2)
-    holder = jnp.sum(jnp.where(lane3 == HALO, ids, 0), axis=2, keepdims=True)
-    seen = jnp.sum(jnp.where((holder == me) & (lane3 < HALO), ids, 0), axis=1)
-    rank = jnp.where(seen > 0, dot(seen.astype(F32).astype(BF), low_tri), -1.0)
-    listed = jnp.concatenate([hal[...], jnp.zeros((HALO, PATCH), I32)], axis=1)
-    listed = jnp.concatenate([listed, jnp.zeros((128 - HALO, 128), I32)], axis=0)
-    listed = listed.T[0:PATCH].astype(F32) + 1.0
-    wide = iota((PATCH, PATCH * RT), 1)
-    mine = wide // RT == iota((PATCH, PATCH * RT), 0)
-    spread = jnp.zeros((PATCH, PATCH * RT), F32)
-    for r in range(RT):
-        node_r = jnp.sum(jnp.where(rank == float(r), listed, 0.0), axis=1, keepdims=True)
-        spread = jnp.where(mine & (lax.rem(wide, RT) == r), node_r, spread)
-    node_of = jnp.sum(spread, axis=0, keepdims=True).astype(I32) - 1
-    amat[...] = hot(iota((NODE, PATCH * RT), 0) == node_of)
     wide_k = iota((1, BLK * RT), 1)
     owner_row = jnp.zeros((1, BLK * RT), I32)
     for b in range(BLK):
@@ -372,10 +403,11 @@
     rid = iota((PATCH * RT, BLK * RT), 0)
     putm[...] = hot((rid // RT == owner_row) & (lax.rem(rid, RT) == lax.rem(wide_k, RT)))
 
-    phase("x5")
-    x_to_z(5)
     phase("z2")
     z_to_d(2)
+    phase("z5w")
+    landed(wz[5])
+    wd[5] = weights_d(5)
     phase("w_edges")
     landed(edges_in)
     landed(vecs)
@@ -385,50 +417,70 @@
     for jr in range(4):
         acc[:, jr * FEAT : (jr + 1) * FEAT] = dot(xe[...], wa[jr, 0]) + vec[pairs[jr], 0:1, :]
     gain = [jnp.concatenate([vec[k, i : i + 1, :] for k in range(4)], axis=1) for i in (1, 2, 4, 5)]
-    phase("z5")
-    z_to_d(5)
-    phase("n34")
+    phase("z7")
+    z_to_d(7)
+    phase("n3")
+    landed(wy[6])
+    wz[6] = weights_round(6)
     wy_to_x(3)
-    wy_to_x(4)
     phase("w_rows0")
     landed(rows_in[0:3])
-    wy[6] = weights_y(6)
     phase("w_d")
     landed(wd[1])
     landed(wd[2])
     landed(wd[5])
+    landed(wd[7])
 
     def norm(mixed, gain_row, shift_row):
         mean = jnp.sum(mixed, axis=1, keepdims=True) * (1.0 / WIDE)
         spread = jnp.sum(mixed * mixed, axis=1, keepdims=True) * (1.0 / WIDE) - mean * mean
         return (mixed - mean) * lax.rsqrt(spread + EPS) * gain_row + shift_row
 
-    section = [dot(xs[TILE : TILE + 2 * HALO, :], wa[k, 2]).astype(BF) for k in range(4)]
+    phase("section")
+    section = [dot(xs[0 : 2 * HALO, :], wa[k, 2]).astype(BF) for k in range(4)]
+    phase("w_rows1")
+    both = jnp.concatenate([rcol[2 * j], rcol[2 * j + 1]], axis=0)
+    lane2 = iota((ROWS, 2 * HALO), 1)
+    base2 = (iota((ROWS, 2 * HALO), 0) // TILE) * HALO
+    take = hot((both >= 0) & (both + base2 == lane2))
+    landed(rows_in[3:6])
+    for u in (4, 8):
+        wy[u] = weights_y(u)
+    phase("edge2a")
+    for k in range(4):
+        cols = slice(k * FEAT, (k + 1) * FEAT)
+        pre = acc[:, cols] + dot(xs[2 * HALO :, :], wa[k, 1]) + dot(take, section[k])
+        hid[:, cols] = silu(pre).astype(BF)
+    phase("x346")
+    phase("edge2b")
+    first = jnp.zeros((ROWS, 1), F32)
+    second = jnp.zeros((ROWS, 1), F32)
+    for n in range(4):
+        cols = slice(n * FEAT, (n + 1) * FEAT)
+        mixed = None
+        for k in range(4):
+            term = dot(hid[:, k * FEAT : (k + 1) * FEAT], wb[k, 0, :, cols]).astype(BF).astype(F32)
+            mixed = term if mixed is None else mixed + term
+        acc[:, cols] = mixed
+        first = first + jnp.sum(mixed, axis=1, keepdims=True)
+        second = second + jnp.sum(mixed * mixed, axis=1, keepdims=True)
+    mean = first * (1.0 / WIDE)
+    scale = lax.rsqrt(second * (1.0 / WIDE) - mean * mean + EPS)
+    member = []
     for bb in range(2):
-        if bb:
-            phase("w_rows1")
-            landed(rows_in[3:6])
-        phase("edge2_%d" % bb)
-        rows = slice(bb * TILE, (bb + 1) * TILE)
-        in_xs = slice(bb * (TILE + 2 * HALO), bb * (TILE + 2 * HALO) + TILE)
-        receiver = rcol[2 * j + bb]
-        take = hot(receiver == iota((TILE, HALO), 1))
-        mixed = None
-        for jr in range(4):
-            cols = slice(jr * FEAT, (jr + 1) * FEAT)
-            pre = acc[rows, cols] + dot(xs[in_xs, :], wa[jr, 1])
-            pre = pre + dot(take, section[jr][bb * HALO : (bb + 1) * HALO, :])
-            hidden = silu(pre).astype(BF)
-            term = dot(hidden, wb[jr, 0]).astype(BF).astype(F32)
-            mixed = term if mixed is None else mixed + term
-        old = xe[rows, :].astype(F32)
-        fresh = jnp.where(receiver >= 0, old + norm(mixed, gain[0], gain[1]), old).astype(BF)
-        outb[rows, :] = fresh
         rank_row = rank8[pl.ds(2 * j + bb, 1), :][:, 0:HALO]
         which = hot(rank_row == iota((RT, HALO), 0).astype(F32))
-        member = hot(rcv[pl.ds(2 * j + bb, 1), :] == iota((HALO, TILE), 0))
-        member = dot(which, member).astype(BF)
-        tsb[bb * RT : (bb + 1) * RT, :] = dot(member, fresh).astype(BF)
+        match = hot(rcv[pl.ds(2 * j + bb, 1), :] == iota((HALO, TILE), 0))
+        member.append(dot(which, match).astype(BF))
+    for n in range(4):
+        cols = slice(n * FEAT, (n + 1) * FEAT)
+        old = xe[:, cols].astype(F32)
+        fresh = (acc[:, cols] - mean) * scale * gain[0][:, cols] + gain[1][:, cols]
+        fresh = jnp.where(both >= 0, old + fresh, old).astype(BF)
+        outb[:, cols] = fresh
+        for bb in range(2):
+            part = dot(member[bb], fresh[bb * TILE : (bb + 1) * TILE, :])
+            tsb[bb * RT : (bb + 1) * RT, cols] = part.astype(BF)
 
     phase("esend")
     my_sums = pl.ds(aligned(j * 2 * RT, 2 * RT), 2 * RT)
@@ -444,6 +496,11 @@
         for dy in (2, 1, 3)
     ])
     tsr[my_sums, :] = tsb[:, my_cols]
+    phase("n36")
+    x_to_z(3)
+    phase("n48")
+    wy_to_x(4)
+    wy_to_x(8)
     phase("w_sums")
     landed(sums)
     phase("sumsend")
@@ -456,6 +513,40 @@
     each_patch(send_sum)
     vv[my_slot, :] = sv[my_slot, :]
 
+    order = (2, 1, 3, 0)
+    half_n = NROW // 2
+
+    def tables():
+        all_ids = pltpu.make_async_copy(idr.at[pl.ds(0, 63)], idr.at[pl.ds(0, 63)], ids_r)
+        all_ids.wait()
+        ids = idr[:, 0, :]
+        bits = [jnp.zeros((PATCH, 1), I32) for _ in range(2)]
+        for b in range(BLK):
+            held = ids[:, b * 16 : b * 16 + 1] == me
+            for k in range(2):
+                bits[k] = jnp.where(held, ids[:, b * 16 + 1 + k : b * 16 + 2 + k], bits[k])
+        lane2 = iota((PATCH, 128), 1)
+        seen = jnp.where(lane2 < 16, bits[0], bits[1])
+        seen = lax.shift_right_logical(seen + jnp.zeros_like(lane2), lax.rem(lane2, 16))
+        seen = jnp.where(lane2 < HALO, lax.rem(seen, 2), 0)
+        rank = jnp.where(seen > 0, dot(seen.astype(F32).astype(BF), low_tri), -1.0)
+        listed = jnp.concatenate([hal[...], jnp.zeros((HALO, PATCH), I32)], axis=1)
+        listed = jnp.concatenate([listed, jnp.zeros((128 - HALO, 128), I32)], axis=0)
+        listed = listed.T[0:PATCH].astype(F32) + 1.0
+        wide = iota((PATCH, PATCH * RT), 1)
+        mine = wide // RT == iota((PATCH, PATCH * RT), 0)
+        spread = jnp.zeros((PATCH, PATCH * RT), F32)
+        for r in range(RT):
+            node_r = jnp.sum(jnp.where(rank == float(r), listed, 0.0), axis=1, keepdims=True)
+            spread = jnp.where(mine & (lax.rem(wide, RT) == r), node_r, spread)
+        node_of = jnp.sum(spread, axis=0, keepdims=True).astype(I32) - 1
+        for h in range(2):
+            for i, dy in enumerate(order):
+                low = (4 * h + i) * half_n
+                node = iota((half_n, PATCH * RT), 0) + (pairs[dy] * NROW + h * half_n)
+                amat[low : low + half_n, :] = hot(node == node_of)
+
+    phase("w_ny")
     phase("eout")
     nodes_in = start([
         rem(
@@ -471,21 +562,23 @@
         )
         for dy in (2, 1, 3)
     ])
-    keep_e = pltpu.make_async_copy(outb.at[:, my_cols], o_e.at[my_edges], loc.at[10])
-    keep_e.start()
-
-    phase("w_ny")
-    wy_to_x(6)
+    o_e[my_edges, :] = outb[:, my_cols]
+    phase("w_n3")
+    z_to_d(3)
+    phase("w_n6")
+    z_to_d(6)
+    phase("w_ids")
+    tables()
     phase("w_nx")
-    for u in (3, 4, 6):
-        x_to_z(u)
+    x_to_z(4)
+    x_to_z(8)
     phase("w_nz")
-    for u in (3, 4, 6):
-        z_to_d(u)
+    z_to_d(4)
+    z_to_d(8)
     phase("w_nin")
     landed(nodes_in)
     phase("w_nd")
-    for u in (3, 4, 6):
+    for u in (3, 4, 6, 8):
         landed(wd[u])
     phase("node1")
     for jr in range(4):
@@ -495,13 +588,12 @@
     got = vv.at[pl.ds(0, 63 * RT)]
     pltpu.make_async_copy(got, got, v2r).wait()
     phase("agg")
-    half_n = NROW // 2
     agg_in = []
     for h in range(2):
         rows = slice(h * half_n, (h + 1) * half_n)
-        for dy in (2, 1, 3, 0):
-            from_rows = pl.ds(aligned(pairs[dy] * NROW + h * half_n, half_n), half_n)
-            part = dot(amat[from_rows, :], vv[...]).astype(BF)
+        parts = dot(amat[4 * h * half_n : 4 * (h + 1) * half_n, :], vv[...]).astype(BF)
+        for i, dy in enumerate(order):
+            part = parts[i * half_n : (i + 1) * half_n, :]
             if dy == 0:
                 xa[rows, my_cols] = part
             else:
@@ -512,7 +604,6 @@
                 ))
                 start(agg_in[-1:])
     nodes_out = []
-    keep_n = []
     for h in range(2):
         phase("w_agg%d" % h)
         landed(agg_in[3 * h : 3 * h + 3])
@@ -535,9 +626,7 @@
             )
             for dy in (2, 1, 3)
         ]))
-        copy = pltpu.make_async_copy(outn.at[rows, my_cols], o_n.at[to_rows], loc.at[11 + h])
-        copy.start()
-        keep_n.append(copy)
+        o_n[to_rows, :] = outn[rows, my_cols]
 
     phase("end_s")
     done = picked.at[pl.ds(0, 63 * HALO)]
@@ -546,9 +635,6 @@
     pltpu.make_async_copy(got, got, v2s).wait()
     for copy in sent:
         copy.wait_send()
-    keep_e.wait()
-    for copy in keep_n:
-        copy.wait()
     phase("end_e")
     landed(edges_out)
     phase("end_n")
@@ -565,28 +651,30 @@
     dma = pltpu.SemaphoreType.DMA
     vm = pltpu.VMEM
     scratch = [
+        pltpu.SMEM((BLK,), I32), pltpu.SMEM((1,), I32), vm((BLK, TILE), I32), vm((BLK, TILE), I32), vm((HALO, PATCH), I32),
         vm((NODE, FEAT), BF), vm((EDGE, 1), I32), vm((EDGE, FEAT), BF), vm((EDGE, FEAT), BF),
-        vm((4, SEL, 1), I32), vm((BLK, TILE, 1), I32), vm((BLK, 128), I32), vm((BLK, 128), F32),
-        vm((PATCH, BLK, 128), I32), vm((4, 8, FEAT), F32), vm((4, SEL, FEAT), F32),
+        vm((4, SEL, 1), I32), vm((BLK, TILE, 1), I32), vm((BLK, 128), I32), vm((1, 128), I32),
+        vm((BLK, 128), F32),
+        vm((PATCH, 1, 128), I32), vm((4, 8, FEAT), F32), vm((4, SEL, FEAT), F32),
         vm((3, SEL, FEAT), BF), vm((SEL, WIDE), BF), vm((ROWS, WIDE), BF), vm((NROW, WIDE), BF),
         vm((4, 5, WIDE, FEAT), BF), vm((4, 2, FEAT, WIDE), BF), vm((WIDE, 2, FEAT), BF),
-        vm((ROWS, WIDE), F32), vm((ROWS, WIDE), BF), vm((2 * RT, WIDE), BF),
+        vm((ROWS, WIDE), F32), vm((ROWS, WIDE), BF), vm((ROWS, WIDE), BF), vm((2 * RT, WIDE), BF),
         vm((BLK * RT, FEAT), BF), vm((PATCH * RT, FEAT), BF), vm((PATCH * RT, FEAT), BF),
         vm((NODE, PATCH * RT), BF), vm((PATCH * RT, BLK * RT), BF), vm((3, NROW, FEAT), BF),
         vm((NROW, WIDE), BF), vm((NROW, WIDE), F32), vm((NROW, WIDE), BF),
-        dma((13,)), dma, dma((4,)), dma, dma, dma((3,)), dma((3,)), dma((3,)), dma((3,)),
-        dma((3,)), dma((3,)), dma((7, 3)), dma((7, 3)), dma((7, 2)), dma((7, 2)), dma((7, 2)),
-        dma((7, 2)), dma((7,)), dma((7,)), dma((2, 3)), dma((2, 3)), dma((3,)), dma((3,)), dma,
+        dma((22,)), dma, dma((4,)), dma, dma, dma((3,)), dma((3,)), dma((3,)), dma((3,)),
+        dma((3,)), dma((3,)), dma((9, 3)), dma((9, 3)), dma((9, 2)), dma((9, 2)), dma((9, 2)),
+        dma((9, 2)), dma((2, 7)), dma((2, 7)), dma((9,)), dma((9,)), dma((2, 3)), dma((2, 3)), dma((3,)), dma((3,)), dma,
         dma, dma((2, 3)), dma((2, 3)), dma((3,)), dma((3,)), dma((2, 3)), dma((2, 3)),
     ]
     return pl.pallas_call(
         kernel,
         out_shape=(
-            jax.ShapeDtypeStruct((NODE, FEAT), BF),
-            jax.ShapeDtypeStruct((EDGE, FEAT), BF),
+            vm((NODE, FEAT), BF),
+            vm((EDGE, FEAT), BF),
         ),
-        in_specs=[ANY, ANY, VM, VM, SM, SM, VM, ANY, ANY, VM, ANY, VM, VM, ANY, VM, ANY, VM, VM],
-        out_specs=(ANY, ANY),
+        in_specs=[ANY] * 18,
+        out_specs=(VM, VM),
         scratch_shapes=scratch,
         compiler_params=pltpu.CompilerParams(
             collective_id=0, has_side_effects=True, vmem_limit_bytes=60 * 2**20

time: 114 us -> 100 us (0.88)
  Pallas kernels: 110 us -> 96.8 us
  local copies, waits for them, and re-layouts: 2.93 us -> 1.77 us
    pallas_call x1, Pallas kernels: 110 us -> 96.8 us  [shards(): pl.pallas_call(kernel, out_shape=(vm((NODE, FEAT), BF), vm((EDGE, FEAT),...]
    unnamed x4 -> x2, local copies, waits for them, and re-layouts: 2.93 us -> 1.77 us
where the time goes in v3:
time: 100 us; the launch traced here: 99.9 us
  Pallas kernels  96.8 us (97%)
  local copies, waits for them, and re-layouts  1.77 us (2%)
  between operations  1.29 us (1%)
    pallas_call x1, Pallas kernels, shards(): pl.pallas_call(kernel, out_shape=(vm((NODE, FEAT), BF), vm((EDGE, FEAT),...  96.8 us

profile of v3, /device:TPU:1, one launch (start us, length us, event | category | flops | bytes accessed | tf_op | source)
XLA Modules:
  0.0 99.9 jit_solution(7153630955658999497)
XLA Ops:
  1.3 96.8 %layer.1 = (bf16[1024,256]{1,0:T(8,128)(2,1)S(1)}, bf16[2048,256]{1,0:T(8,128)(2,1)S(1)}) custom-call(bf16[1024,256]{1,0:T(8,128)(2,1)} %nl.1, bf16[2048,256]{1,0:T(8,128)(2,1)} %el.1, s32[8,256]{1,0:T(8,128)} %snd_h.1, s32[8,256]{1,0:T(8,128)} %rcv_h.1, s32[8]{0:T(128)} %own_h.1, s32[1]{0:T(128)S(6)} %copy.24.cnt_h, s32[32,64]{1,0:T(8,128)} %bitcast.9, ...), custom_call_target="tpu_custom_call" | custom-call | tf_op jit(solution)/shard_map/layer/pallas_call | solution.py:670
  98.1 0.8 copy.22
  98.9 1.0 copy.23

commit v4 on v3

--- a/solution.py
+++ b/solution.py
@@ -501,6 +501,20 @@
     phase("n48")
     wy_to_x(4)
     wy_to_x(8)
+    nodes_in = start([
+        rem(
+            nl.at[pl.ds(aligned(pairs[dy] * NROW, NROW), NROW)], xn.at[:, my_cols],
+            xns.at[dy - 1], xnr.at[dy - 1], (me, pairs[dy]),
+        )
+        for dy in (2, 1, 3)
+    ])
+    edges_out = start([
+        rem(
+            outb.at[:, cols_of(dy)], o_e.at[my_edges], oes.at[dy - 1], oer.at[dy - 1],
+            (me, pairs[dy]),
+        )
+        for dy in (2, 1, 3)
+    ])
     phase("w_sums")
     landed(sums)
     phase("sumsend")
@@ -548,20 +562,6 @@
 
     phase("w_ny")
     phase("eout")
-    nodes_in = start([
-        rem(
-            nl.at[pl.ds(aligned(pairs[dy] * NROW, NROW), NROW)], xn.at[:, my_cols],
-            xns.at[dy - 1], xnr.at[dy - 1], (me, pairs[dy]),
-        )
-        for dy in (2, 1, 3)
-    ])
-    edges_out = start([
-        rem(
-            outb.at[:, cols_of(dy)], o_e.at[my_edges], oes.at[dy - 1], oer.at[dy - 1],
-            (me, pairs[dy]),
-        )
-        for dy in (2, 1, 3)
-    ])
     o_e[my_edges, :] = outb[:, my_cols]
     phase("w_n3")
     z_to_d(3)
@@ -572,14 +572,10 @@
     phase("w_nx")
     x_to_z(4)
     x_to_z(8)
-    phase("w_nz")
-    z_to_d(4)
-    z_to_d(8)
     phase("w_nin")
     landed(nodes_in)
     phase("w_nd")
-    for u in (3, 4, 6, 8):
-        landed(wd[u])
+    landed(wd[3])
     phase("node1")
     for jr in range(4):
         acc2[:, jr * FEAT : (jr + 1) * FEAT] = dot(xn[...], wa[jr, 3]) + vec[pairs[jr], 3:4, :]
@@ -603,6 +599,12 @@
                     ar_.at[h, dy - 1], (me, pairs[dy]),
                 ))
                 start(agg_in[-1:])
+    phase("w_nz")
+    z_to_d(4)
+    z_to_d(8)
+    phase("w_nd2")
+    for u in (6, 4, 8):
+        landed(wd[u])
     nodes_out = []
     for h in range(2):
         phase("w_agg%d" % h)

time: 100 us -> 97.3 us (0.973)
  Pallas kernels: 96.8 us -> 93.8 us
    pallas_call x1, Pallas kernels: 96.8 us -> 93.8 us  [shards(): pl.pallas_call(kernel, out_shape=(vm((NODE, FEAT), BF), vm((EDGE, FEAT),...]
where the time goes in v4:
time: 97.3 us; the launch traced here: 96.9 us
  Pallas kernels  93.8 us (96%)
  local copies, waits for them, and re-layouts  1.77 us (2%)
  between operations  1.29 us (1%)
    pallas_call x1, Pallas kernels, shards(): pl.pallas_call(kernel, out_shape=(vm((NODE, FEAT), BF), vm((EDGE, FEAT),...  93.8 us

profile of v4, /device:TPU:1, one launch (start us, length us, event | category | flops | bytes accessed | tf_op | source)
XLA Modules:
  0.0 96.9 jit_solution(8967818640177868914)
XLA Ops:
  1.3 93.8 %layer.1 = (bf16[1024,256]{1,0:T(8,128)(2,1)S(1)}, bf16[2048,256]{1,0:T(8,128)(2,1)S(1)}) custom-call(bf16[1024,256]{1,0:T(8,128)(2,1)} %nl.1, bf16[2048,256]{1,0:T(8,128)(2,1)} %el.1, s32[8,256]{1,0:T(8,128)} %snd_h.1, s32[8,256]{1,0:T(8,128)} %rcv_h.1, s32[8]{0:T(128)} %own_h.1, s32[1]{0:T(128)S(6)} %copy.24.cnt_h, s32[32,64]{1,0:T(8,128)} %bitcast.9, ...), custom_call_target="tpu_custom_call" | custom-call | tf_op jit(solution)/shard_map/layer/pallas_call | solution.py:672
  95.1 0.8 copy.22
  95.9 1.0 %copy.23 = bf16[2048,256]{1,0:T(8,128)(2,1)} copy(bf16[2048,256]{1,0:T(8,128)(2,1)S(1)} %get-tuple-element.3) | data formatting | bytes 2097152

commit v5 on v4

--- a/solution.py
+++ b/solution.py
@@ -24,7 +24,7 @@
 SEL = ROWS + 2 * HALO
 NROW = NODE // 4
 PICK = 2
-CUT = 512
+CUT = (512, 640)
 ANY = pl.BlockSpec(memory_space=pl.ANY)
 VM = pl.BlockSpec(memory_space=pltpu.VMEM)
 
@@ -180,12 +180,14 @@
         if u < 5:
             return wa.at[js, u, pl.ds(aligned(base * 128 + low * 64, 64), size * 64)]
         rows = pl.ds(aligned(base * 32 + low * 16, 16), size * 16)
-        cols = pl.ds(0, CUT) if u < 7 else pl.ds(CUT, WIDE - CUT)
-        return wb.at[js, (u + 1) % 2, rows, cols]
+        b = (u + 1) % 2
+        cols = pl.ds(0, CUT[b]) if u < 7 else pl.ds(CUT[b], WIDE - CUT[b])
+        return wb.at[js, b, rows, cols]
 
     def thin(u, js):
         rows = pl.ds(aligned((c * 8 + z) * 16, 16), 16)
-        return wb.at[js, (u + 1) % 2, rows, pl.ds(0, CUT)]
+        b = (u + 1) % 2
+        return wb.at[js, b, rows, pl.ds(0, CUT[b])]
 
     others = pl.ds(1, 3)
 

time: 97.3 us -> 96.9 us (level)
  no operation moved by 1% of the time
where the time goes in v5:
time: 96.9 us; the launch traced here: 96.3 us
  Pallas kernels  93.3 us (96%)
  local copies, waits for them, and re-layouts  1.77 us (2%)
  between operations  1.29 us (1%)
    pallas_call x1, Pallas kernels, shards(): pl.pallas_call(kernel, out_shape=(vm((NODE, FEAT), BF), vm((EDGE, FEAT),...  93.3 us

profile of v5, /device:TPU:1, one launch (start us, length us, event | category | flops | bytes accessed | tf_op | source)
XLA Modules:
  0.0 96.3 jit_solution(2030207144816234061)
XLA Ops:
  1.3 93.3 %layer.1 = (bf16[1024,256]{1,0:T(8,128)(2,1)S(1)}, bf16[2048,256]{1,0:T(8,128)(2,1)S(1)}) custom-call(bf16[1024,256]{1,0:T(8,128)(2,1)} %nl.1, bf16[2048,256]{1,0:T(8,128)(2,1)} %el.1, s32[8,256]{1,0:T(8,128)} %snd_h.1, s32[8,256]{1,0:T(8,128)} %rcv_h.1, s32[8]{0:T(128)} %own_h.1, s32[1]{0:T(128)S(6)} %copy.24.cnt_h, s32[32,64]{1,0:T(8,128)} %bitcast.9, ...), custom_call_target="tpu_custom_call" | custom-call | tf_op jit(solution)/shard_map/layer/pallas_call | solution.py:674
  94.6 0.8 copy.22
  95.4 1.0 %copy.23 = bf16[2048,256]{1,0:T(8,128)(2,1)} copy(bf16[2048,256]{1,0:T(8,128)(2,1)S(1)} %get-tuple-element.3) | data formatting | bytes 2097152
